TPU v7x, 32 devices: a whole 2x2x4 slice. The times are simulated.
32 devices in a mesh: tm: 4 (over y, core), lat: 8 (over z, x).
Axes of the slice: x: 2, y: 2, z: 4, core: 2. Of those that a mesh axis runs over, the one named last changes fastest.
Arguments:
- trajectory: float32 [4, 32, 64, 2048], P('tm', 'lat'), may hold values from -6 to 6
- diffusivity: float32 [4, 32, 64, 2048], P('tm', 'lat'), may hold values from 0.02 to 0.24
- adjoint_end: bfloat16 [32, 64, 2048], P('lat'), may hold values from -6 to 6
- obs_jac: bfloat16 [3072, 128, 128], P(('tm', 'lat')), may hold values from -0.5 to 0.5
- obs_value: float32 [3072, 128], P(('tm', 'lat')), may hold values from -6 to 6
- obs_weight: float32 [3072, 128], P(('tm', 'lat')), may hold values from 0.3 to 3
- obs_valid: int32 [3072, 128], P(('tm', 'lat')), may hold values 0 or 1
- obs_owner: int32 [3072, 1], P(('tm', 'lat')), may hold values from 0 to 31; in each aligned block of 96 rows (0 to 95, 96 to 191, ...) at most 6 rows name the same one
- obs_tile: int32 [3072], P(('tm', 'lat')), may hold values from 0 to 4095
Outputs:
- adjoint: float32 [4, 32, 64, 2048], P('tm', 'lat')
Inputs may be any that keep to these rules, and one draw needn't show every extreme that they name: `obs_owner`: among the 96 blocks of one device, no owner is named more than 6 times, a bound that some block reaches.
All inputs are finite; a program needn't handle non-finite values. No bound on the sum of `obs_valid` on one device may be relied on, other than what follows from the above.
Results may differ from a plain program's by a relative error of at most 0.0024.
Values may be sent and summed in bfloat16 or wider, within the bound.
A program may use at most 128 MiB of HBM per device.

v0:
```python
import functools

import jax
import jax.numpy as jnp
from jax import lax
from jax.experimental import pallas as pl
from jax.experimental.pallas import tpu as pltpu
from jax.sharding import PartitionSpec as P

TW = 2
SUB = 2
LANES = 128
PAD = 8
CHUNK = 8
MESH = pl.DeviceIdType.MESH
VMEM = pl.BlockSpec(memory_space=pltpu.VMEM)
SMEM = pl.BlockSpec(memory_space=pltpu.SMEM)


def route_kernel(slots, owner_ref, tile_ref, ids_ref, slot_ref, count_ref):
    devices = ids_ref.shape[0]

    def clear(d, carry):
        count_ref[d] = 0
        for s in range(slots):
            ids_ref[d, s] = 0
        return carry

    lax.fori_loop(0, devices, clear, 0)

    def place(k, carry):
        target = owner_ref[k]
        rank = count_ref[target]
        count_ref[target] = rank + 1
        ids_ref[target, rank] = tile_ref[k]
        slot_ref[k] = target * PAD + rank
        return carry

    lax.fori_loop(0, owner_ref.shape[0], place, 0)


def route(owner, tile, devices, slots):
    return pl.pallas_call(
        functools.partial(route_kernel, slots),
        out_shape=(
            jax.ShapeDtypeStruct((devices, LANES), jnp.int32),
            jax.ShapeDtypeStruct(owner.shape, jnp.int32),
        ),
        in_specs=[SMEM, SMEM],
        out_specs=(SMEM, SMEM),
        scratch_shapes=[pltpu.SMEM((devices,), jnp.int32)],
        name="route",
    )(owner, tile)


def exchange_kernel(count, lat, shift, *refs):
    if shift:
        x_ref, edge_ref, out_ref, beside_ref, send_sem, recv_sem, own_sem, edge_send, edge_recv = refs
    else:
        x_ref, out_ref, send_sem, recv_sem, own_sem = refs
    me = lax.axis_index("tm") * lat + lax.axis_index("lat")
    barrier = pltpu.get_barrier_semaphore()

    def greet(j, carry):
        to = lax.rem(me + j, count)
        pl.semaphore_signal(barrier, inc=1, device_id=(to // lat, lax.rem(to, lat)), device_id_type=MESH)
        return carry

    lax.fori_loop(1, count, greet, 0)
    own = pltpu.make_async_copy(x_ref.at[me], out_ref.at[me], own_sem)
    own.start()
    pl.semaphore_wait(barrier, count - 1)

    def outgoing(j):
        to = lax.rem(me + j, count)
        return pltpu.make_async_remote_copy(
            src_ref=x_ref.at[to],
            dst_ref=out_ref.at[me],
            send_sem=send_sem.at[j],
            recv_sem=recv_sem.at[j],
            device_id=(to // lat, lax.rem(to, lat)),
            device_id_type=MESH,
        )

    def incoming(j):
        source = lax.rem(me + count - j, count)
        return pltpu.make_async_remote_copy(
            src_ref=x_ref.at[source],
            dst_ref=out_ref.at[source],
            send_sem=send_sem.at[j],
            recv_sem=recv_sem.at[j],
            device_id=(source // lat, lax.rem(source, lat)),
            device_id_type=MESH,
        )

    def launch(j, carry):
        outgoing(j).start()
        return carry

    def land(j, carry):
        incoming(j).wait_recv()
        outgoing(j).wait_send()
        return carry

    lax.fori_loop(1, count, launch, 0)
    if shift:
        band, section = lax.axis_index("lat"), lax.axis_index("tm")
        is_last = section == count // lat - 1
        gives = is_last & (band < lat - 1 if shift > 0 else band > 0)
        takes = is_last & (band > 0 if shift > 0 else band < lat - 1)

        def edge():
            return pltpu.make_async_remote_copy(
                src_ref=edge_ref,
                dst_ref=beside_ref,
                send_sem=edge_send,
                recv_sem=edge_recv,
                device_id=(section, band + shift),
                device_id_type=MESH,
            )

        @pl.when(gives)
        def _():
            edge().start()

        @pl.when(jnp.logical_not(takes))
        def _():
            beside_ref[...] = jnp.zeros_like(beside_ref)

    own.wait()
    lax.fori_loop(1, count, land, 0)
    if shift:
        @pl.when(takes)
        def _():
            edge().wait_recv()

        @pl.when(gives)
        def _():
            edge().wait_send()


def last_edges_kernel(coeff_ref, end_ref, low_ref, high_ref, first_ref, final_ref):
    rows, levels, nlon = end_ref.shape

    def one(c, carry):
        span = pl.ds(pl.multiple_of(c * 16, 16), 16)

        def weigh(r):
            return coeff_ref[0, r, span, :] * end_ref[r, span, :].astype(jnp.float32)

        for r, inner, ref in ((0, 1, low_ref), (rows - 1, rows - 2, high_ref)):
            mid = weigh(r)
            value = end_ref[r, span, :].astype(jnp.float32) + weigh(inner)
            value = value + pltpu.roll(mid, 1, 1) + pltpu.roll(mid, nlon - 1, 1) - 4.0 * mid
            ref[0, span, :] = mid.astype(jnp.bfloat16)
            ref[1, span, :] = (coeff_ref[0, r, span, :] * value).astype(jnp.bfloat16)
        first_ref[0, span, :] = coeff_ref[0, 0, span, :].astype(jnp.bfloat16)
        final_ref[0, span, :] = coeff_ref[0, rows - 1, span, :].astype(jnp.bfloat16)
        return carry

    lax.fori_loop(0, levels // 16, one, 0)


def last_edges(coeff, end):
    edge = jax.ShapeDtypeStruct((2,) + end.shape[1:], jnp.bfloat16)
    single = jax.ShapeDtypeStruct((1,) + end.shape[1:], jnp.bfloat16)
    return pl.pallas_call(
        last_edges_kernel,
        out_shape=(edge, edge, single, single),
        in_specs=[VMEM, VMEM],
        out_specs=(VMEM,) * 4,
        name="last_edges",
    )(coeff, end)


def exchange(x, collective_id, edge=None, shift=0):
    lat = lax.axis_size("lat")
    count = lax.axis_size("tm") * lat
    if shift:
        return pl.pallas_call(
            functools.partial(exchange_kernel, count, lat, shift),
            out_shape=(jax.ShapeDtypeStruct(x.shape, x.dtype), jax.ShapeDtypeStruct(edge.shape, edge.dtype)),
            in_specs=[VMEM, VMEM],
            out_specs=(VMEM, VMEM),
            scratch_shapes=[pltpu.SemaphoreType.DMA((count,))] * 2 + [pltpu.SemaphoreType.DMA] * 3,
            compiler_params=pltpu.CompilerParams(collective_id=collective_id, has_side_effects=True),
            name="exchange%d" % collective_id,
        )(x, edge)
    return pl.pallas_call(
        functools.partial(exchange_kernel, count, lat, 0),
        out_shape=jax.ShapeDtypeStruct(x.shape, x.dtype),
        in_specs=[VMEM],
        out_specs=VMEM,
        scratch_shapes=[
            pltpu.SemaphoreType.DMA((count,)),
            pltpu.SemaphoreType.DMA((count,)),
            pltpu.SemaphoreType.DMA,
        ],
        compiler_params=pltpu.CompilerParams(collective_id=collective_id, has_side_effects=True),
        name="exchange%d" % collective_id,
    )(x)


def tile_place(tile, per_row):
    row = tile // per_row
    lon = (tile - row * per_row) * TW
    column = lon // LANES
    return row, pl.multiple_of(column * LANES, LANES), lon - column * LANES


def gather_kernel(slots, ids_ref, traj_ref, out_ref):
    _, _, levels, nlon = traj_ref.shape
    per_row = nlon // TW
    tile_len = levels * TW
    entry = lax.broadcasted_iota(jnp.int32, (levels, tile_len), 1)
    level = lax.broadcasted_iota(jnp.int32, (levels, tile_len), 0)
    part = lax.rem(entry, TW)
    keep = entry // TW == level
    zeros = jnp.zeros((PAD - slots, tile_len), jnp.float32)

    def one(d, carry):
        rows = []
        for s in range(slots):
            row, start, offset = tile_place(ids_ref[d, s], per_row)
            field = traj_ref[0, row, :, pl.ds(start, LANES)]
            picked = jnp.take_along_axis(field, part + offset, axis=1)
            rows.append(jnp.sum(jnp.where(keep, picked, 0.0), axis=0, keepdims=True))
        out_ref[d] = jnp.concatenate(rows + [zeros], axis=0)
        return carry

    lax.fori_loop(0, out_ref.shape[0], one, 0)


def gather(ids, traj, slots):
    devices = ids.shape[0]
    tile_len = traj.shape[2] * TW
    return pl.pallas_call(
        functools.partial(gather_kernel, slots),
        out_shape=jax.ShapeDtypeStruct((devices, PAD, tile_len), jnp.float32),
        in_specs=[SMEM, VMEM],
        out_specs=VMEM,
        name="gather",
    )(ids, traj)


def split(x):
    top = x.astype(jnp.bfloat16)
    rest = (x - top.astype(jnp.float32)).astype(jnp.bfloat16)
    return jnp.concatenate([top, rest], axis=0)


def blocks_kernel(slot_ref, state_ref, jac_ref, value_ref, weight_ref, valid_ref, out_ref):
    group = PAD
    blocks, _, tile_len = jac_ref.shape
    out_ref[...] = jnp.zeros_like(out_ref)
    rank = lax.rem(lax.broadcasted_iota(jnp.int32, (2 * group, tile_len), 0), group)

    def product(vectors, first, dims):
        both = split(vectors)
        picked = jnp.zeros((2 * group, tile_len), jnp.float32)
        for i in range(group):
            full = lax.dot_general(both, jac_ref[first + i], dims, preferred_element_type=jnp.float32)
            picked = jnp.where(rank == i, full, picked)
        return picked[:group] + picked[group:]

    def one(g, carry):
        first = pl.multiple_of(g * group, group)
        places = [slot_ref[first + i] for i in range(group)]
        states = jnp.concatenate([state_ref[pl.ds(p, 1), :] for p in places], axis=0)
        here = pl.ds(first, group)
        pred = product(states, first, (((1,), (1,)), ((), ())))
        weight = weight_ref[here, :] * valid_ref[here, :].astype(jnp.float32)
        terms = product(weight * (value_ref[here, :] - pred), first, (((1,), (0,)), ((), ())))
        for i, p in enumerate(places):
            out_ref[pl.ds(p, 1), :] = terms[i : i + 1]
        return carry

    lax.fori_loop(0, blocks // group, one, 0)


def block_terms(slot, states, jac, value, weight, valid):
    return pl.pallas_call(
        blocks_kernel,
        out_shape=jax.ShapeDtypeStruct(states.shape, jnp.float32),
        in_specs=[SMEM] + [VMEM] * 5,
        out_specs=VMEM,
        name="blocks",
    )(slot, states, jac, value, weight, valid)


def scatter_kernel(slots, ids_ref, terms_ref, out_ref):
    _, levels, nlon = out_ref.shape
    per_row = nlon // TW
    out_ref[...] = jnp.zeros_like(out_ref)
    lane = lax.broadcasted_iota(jnp.int32, (levels, LANES), 1)
    level = lax.broadcasted_iota(jnp.int32, (levels, LANES), 0)
    source = level * TW + lax.rem(lane, TW)
    owner = lane // TW

    def one(d, carry):
        for s in range(slots):
            row, start, offset = tile_place(ids_ref[d, s], per_row)
            spread = jnp.broadcast_to(terms_ref[d, s : s + 1, :], (levels, levels * TW))
            moved = jnp.take_along_axis(spread, source, axis=1)
            here = (row, slice(None), pl.ds(start, LANES))
            out_ref[here] = out_ref[here] + jnp.where(owner == offset // TW, moved, 0.0)
        return carry

    lax.fori_loop(0, terms_ref.shape[0], one, 0)


def scatter(ids, terms, shape, slots):
    return pl.pallas_call(
        functools.partial(scatter_kernel, slots),
        out_shape=jax.ShapeDtypeStruct(shape, jnp.float32),
        in_specs=[SMEM, VMEM],
        out_specs=VMEM,
        name="scatter",
    )(ids, terms)


def chain_kernel(
    sections, lats, coeff_ref, low_ref, high_ref, last_low_ref, last_high_ref, end_ref, forcing_ref, out_ref,
    main, low, high, edge_low, edge_high, ahead, weighted, partial, second,
    main_send, main_recv, down_send, up_send, low_recv, high_recv,
):
    section, band = lax.axis_index("tm"), lax.axis_index("lat")
    rows, levels, nlon = end_ref.shape
    chunks = levels // CHUNK
    is_last = section == sections - 1
    has_before, has_low, has_high = section > 0, band > 0, band < lats - 1

    sends_low, sends_high = has_low & jnp.logical_not(is_last), has_high & jnp.logical_not(is_last)

    barrier = pltpu.get_barrier_semaphore()
    sides = (
        (jnp.logical_not(is_last), section + 1, band),
        (has_before, section - 1, band),
        (has_low, section, band - 1),
        (has_high, section, band + 1),
    )
    for there, tm, lat in sides:
        @pl.when(there)
        def _(tm=tm, lat=lat):
            pl.semaphore_signal(barrier, inc=1, device_id=(tm, lat), device_id_type=MESH)
    pl.semaphore_wait(barrier, sum(there.astype(jnp.int32) for there, _, _ in sides))

    def remote(src, dst, send, recv, tm, lat):
        return pltpu.make_async_remote_copy(
            src_ref=src, dst_ref=dst, send_sem=send, recv_sem=recv, device_id=(tm, lat), device_id_type=MESH
        )

    def local_main(c):
        return pltpu.make_async_copy(
            end_ref.at[:, pl.ds(pl.multiple_of(c * CHUNK, CHUNK), CHUNK), :], main.at[c], main_recv.at[c]
        )

    def handed(c):
        return remote(ahead.at[c], main.at[c], main_send.at[c], main_recv.at[c], section - 1, band)

    def downward(c):
        return remote(edge_low.at[c], high.at[c], down_send.at[c], high_recv.at[c], section, band - 1)

    def upward(c):
        return remote(edge_high.at[c], low.at[c], up_send.at[c], low_recv.at[c], section, band + 1)

    @pl.when(jnp.logical_not(has_low))
    def _():
        low[...] = jnp.zeros_like(low)

    @pl.when(jnp.logical_not(has_high))
    def _():
        high[...] = jnp.zeros_like(high)

    @pl.when(is_last)
    def _():
        for c in range(chunks):
            local_main(c).start()
            low[c] = last_low_ref[:, c * CHUNK : (c + 1) * CHUNK, :]
            high[c] = last_high_ref[:, c * CHUNK : (c + 1) * CHUNK, :]

    def levels_of(c):
        return pl.ds(pl.multiple_of(c * CHUNK, CHUNK), CHUNK)

    def along(mid):
        return pltpu.roll(mid, 1, 1) + pltpu.roll(mid, nlon - 1, 1) - 4.0 * mid

    def begin(c):
        @pl.when(is_last)
        def _():
            local_main(c).wait()

        @pl.when(jnp.logical_not(is_last))
        def _():
            handed(c).wait_recv()

        span = levels_of(c)
        for r in range(rows):
            weighted[c, r] = coeff_ref[0, r, span, :] * main[c, r].astype(jnp.float32)
        for r in range(rows):
            mid = weighted[c, r]
            value = main[c, r].astype(jnp.float32) + along(mid)
            if r > 0:
                value = value + weighted[c, r - 1]
            if r < rows - 1:
                value = value + weighted[c, r + 1]
            partial[c, r] = value
            if r == 0:
                edge_low[c, 0] = mid.astype(jnp.bfloat16)
                edge_low[c, 1] = (coeff_ref[0, r, span, :] * value).astype(jnp.bfloat16)
            if r == rows - 1:
                edge_high[c, 0] = mid.astype(jnp.bfloat16)
                edge_high[c, 1] = (coeff_ref[0, r, span, :] * value).astype(jnp.bfloat16)

        @pl.when(sends_low)
        def _():
            downward(c).start()

        @pl.when(sends_high)
        def _():
            upward(c).start()

    def complete(c):
        span = levels_of(c)
        end = rows - 1
        partial[c, 0] = partial[c, 0] + low[c, 0].astype(jnp.float32)
        partial[c, end] = partial[c, end] + high[c, 0].astype(jnp.float32)
        second[0] = low[c, 1].astype(jnp.float32) + low_ref[0, span, :].astype(jnp.float32) * weighted[c, 0]
        second[rows + 1] = high[c, 1].astype(jnp.float32) + high_ref[0, span, :].astype(jnp.float32) * weighted[c, end]
        for r in range(rows):
            second[r + 1] = coeff_ref[0, r, span, :] * partial[c, r]
        for r in range(rows):
            value = partial[c, r] + second[r] + second[r + 2] + along(second[r + 1]) + forcing_ref[r, span, :]
            out_ref[0, r, span, :] = value
            ahead[c, r] = value.astype(jnp.bfloat16)

    look = jnp.where(section == sections - 2, min(4, chunks), min(2, chunks))

    def open_one(c, carry):
        begin(c)
        return carry

    lax.fori_loop(0, look, open_one, 0)

    def step(c, carry):
        @pl.when(c + look < chunks)
        def _():
            begin(c + look)

        @pl.when(sends_low)
        def _():
            upward(c).wait_recv()

        @pl.when(sends_high)
        def _():
            downward(c).wait_recv()

        complete(c)

        @pl.when(has_before)
        def _():
            handed(c).start()

        return carry

    lax.fori_loop(0, chunks, step, 0)

    def finish(c, carry):
        @pl.when(sends_low)
        def _():
            downward(c).wait_send()

        @pl.when(sends_high)
        def _():
            upward(c).wait_send()

        @pl.when(has_before)
        def _():
            handed(c).wait_send()

        return carry

    lax.fori_loop(0, chunks, finish, 0)


def chain(coeff, low, high, last_low, last_high, end, forcing):
    rows, levels, nlon = end.shape
    chunks = levels // CHUNK
    part = lambda n, kind: pltpu.VMEM((chunks, n, CHUNK, nlon), kind)
    return pl.pallas_call(
        functools.partial(chain_kernel, lax.axis_size("tm"), lax.axis_size("lat")),
        out_shape=jax.ShapeDtypeStruct(coeff.shape, jnp.float32),
        in_specs=[VMEM] * 7,
        out_specs=VMEM,
        scratch_shapes=[
            part(rows, jnp.bfloat16),
            part(SUB, jnp.bfloat16),
            part(SUB, jnp.bfloat16),
            part(SUB, jnp.bfloat16),
            part(SUB, jnp.bfloat16),
            part(rows, jnp.bfloat16),
            part(rows, jnp.float32),
            part(rows, jnp.float32),
            pltpu.VMEM((rows + 2, CHUNK, nlon), jnp.float32),
        ]
        + [pltpu.SemaphoreType.DMA((chunks,))] * 6,
        compiler_params=pltpu.CompilerParams(
            collective_id=9, has_side_effects=True, vmem_limit_bytes=48 * 1024 * 1024
        ),
        name="chain",
    )(coeff, low, high, last_low, last_high, end, forcing)


def per_device(
    trajectory,
    diffusivity,
    adjoint_end,
    obs_jac,
    obs_value,
    obs_weight,
    obs_valid,
    obs_owner,
    obs_tile,
):
    _, lat_dev, levels, nlon = trajectory.shape
    lats = lax.axis_size("lat")
    devices = lax.axis_size("tm") * lats
    blocks = obs_owner.shape[0]
    slots = max(2, 2 * blocks // devices)
    upward = [(i, i + 1) for i in range(lats - 1)]
    downward = [(i + 1, i) for i in range(lats - 1)]
    ids, slot = route(obs_owner[:, 0], obs_tile, devices, slots)
    wanted = exchange(ids[:, None, :], 1)[:, 0]
    edge_low, edge_high, first_row, final_row = last_edges(diffusivity, adjoint_end)
    edges = lax.optimization_barrier((first_row, final_row, wanted))
    wanted = edges[2]
    low = lax.ppermute(edges[1], "lat", upward)
    high = lax.ppermute(edges[0], "lat", downward)
    found = gather(wanted, trajectory, slots)
    returned, last_low = exchange(found, 2, edge_high, 1)
    terms = block_terms(
        slot, returned.reshape(devices * PAD, -1), obs_jac, obs_value, obs_weight, obs_valid
    )
    received, last_high = exchange(terms.reshape(found.shape), 3, edge_low, -1)
    forcing = scatter(wanted, received, (lat_dev, levels, nlon), slots)
    return chain(diffusivity, low, high, last_low, last_high, adjoint_end, forcing)


def solution(mesh):
    in_specs = (
        P("tm", "lat", None, None),
        P("tm", "lat", None, None),
        P("lat", None, None),
        P(("tm", "lat"), None, None),
        P(("tm", "lat"), None),
        P(("tm", "lat"), None),
        P(("tm", "lat"), None),
        P(("tm", "lat"), None),
        P(("tm", "lat")),
    )
    out_specs = P("tm", "lat", None, None)
    return jax.shard_map(
        per_device, mesh=mesh, in_specs=in_specs, out_specs=out_specs, check_vma=False
    )
```

profile of v0, /device:TPU:8, one launch (start us, length us, event | category | flops | bytes accessed | tf_op | source)
XLA Modules:
  0.0 122.5 jit_solution(8593048024827132134)
XLA Ops:
  0.0 2.7 %route.1 = (s32[32,128]{1,0:T(8,128)}, s32[96]{0:T(128)}) custom-call(s32[96]{0:T(128)} %bitcast.10, s32[96]{0:T(128)} %tile_ref.1), custom_call_target="tpu_custom_call" | custom-call | tf_op jit(solution)/shard_map/route/pallas_call | solution.py:43
  2.7 9.7 %exchange1.1 = s32[32,1,128]{2,1,0:T(1,128)} custom-call(s32[32,1,128]{2,1,0:T(1,128)} %bitcast.9), custom_call_target="tpu_custom_call" | custom-call | tf_op jit(solution)/shard_map/exchange1/pallas_call | solution.py:189
  12.4 3.8 %last_edges.1 = (bf16[2,64,2048]{2,1,0:T(8,128)(2,1)}, bf16[2,64,2048]{2,1,0:T(8,128)(2,1)}, bf16[1,64,2048]{2,1,0:T(8,128)(2,1)}, bf16[1,64,2048]{2,1,0:T(8,128)(2,1)}) custom-call(f32[1,4,64,2048]{3,2,1,0:T(8,128)} %coeff_ref.3, bf16[4,64,2048]{2,1,0:T(8,128)(2,1)} %end_ref.3), custom_call_target="tpu_custom_call" | custom-call | tf_op jit(solution)/shard_map/last_edges/pallas_call | solution.py:167
  16.2 3.3 %collective-permute-start = (bf16[1,64,2048]{2,1,0:T(8,128)(2,1)}, bf16[1,64,2048]{2,1,0:T(8,128)(2,1)S(1)}, u32[]{:S(2)}, u32[]{:S(2)}) collective-permute-start(bf16[1,64,2048]{2,1,0:T(8,128)(2,1)} %get-tuple-element.21), channel_id=1, source_target_pairs={{0,1},{1,2},{2,3},{3,4},{4,5},{5,6},{6,7},{8,9},{9,10},{10,11},{11... | collective-permute-start | bytes 786440 | tf_op jit(solution)/shard_map/ppermute | solution.py:537
  19.6 3.4 %collective-permute-start.1 = (bf16[1,64,2048]{2,1,0:T(8,128)(2,1)}, bf16[1,64,2048]{2,1,0:T(8,128)(2,1)S(1)}, u32[]{:S(2)}, u32[]{:S(2)}) collective-permute-start(bf16[1,64,2048]{2,1,0:T(8,128)(2,1)} %get-tuple-element.22), channel_id=1, source_target_pairs={{1,0},{2,1},{3,2},{4,3},{5,4},{6,5},{7,6},{9,8},{10,9},{11,10},{12... | collective-permute-start | bytes 786440 | tf_op jit(solution)/shard_map/ppermute | solution.py:538
  23.0 8.7 %gather.1.refs_0_ = f32[32,8,128]{2,1,0:T(8,128)} custom-call(s32[32,128]{1,0:T(8,128)} %bitcast.6, f32[1,4,64,2048]{3,2,1,0:T(8,128)} %traj_ref.1), custom_call_target="tpu_custom_call" | custom-call | tf_op jit(solution)/shard_map/gather/pallas_call | solution.py:237
  31.6 11.0 %exchange2.1 = (f32[32,8,128]{2,1,0:T(8,128)}, bf16[2,64,2048]{2,1,0:T(8,128)(2,1)}) custom-call(f32[32,8,128]{2,1,0:T(8,128)} %gather.1.refs_0_, bf16[2,64,2048]{2,1,0:T(8,128)(2,1)} %get-tuple-element.24.refs_1_), custom_call_target="tpu_custom_call" | custom-call | tf_op jit(solution)/shard_map/exchange2/pallas_call | solution.py:180
  42.6 7.8 %blocks.1 = f32[256,128]{1,0:T(8,128)} custom-call(s32[96]{0:T(128)} %get-tuple-element.26.slot_ref, f32[256,128]{1,0:T(8,128)} %bitcast.8, bf16[96,128,128]{2,1,0:T(8,128)(2,1)} %jac_ref.1, f32[96,128]{1,0:T(8,128)} %value_ref.1, f32[96,128]{1,0:T(8,128)} %weight_ref.1, s32[96,128]{1,0:T(8,128)} %valid_ref.1), custom_call_target="tpu_custom_call" | custom-call | tf_op jit(solution)/shard_map/blocks/pallas_call | solution.py:282
  50.4 0.0 copy-start
  50.4 0.0 copy-start.1
  50.4 14.8 %exchange3.1 = (f32[32,8,128]{2,1,0:T(8,128)}, bf16[2,64,2048]{2,1,0:T(8,128)(2,1)}) custom-call(f32[32,8,128]{2,1,0:T(8,128)} %bitcast.5, bf16[2,64,2048]{2,1,0:T(8,128)(2,1)} %get-tuple-element.28.refs_1_), custom_call_target="tpu_custom_call" | custom-call | tf_op jit(solution)/shard_map/exchange3/pallas_call | solution.py:180
  65.2 0.0 copy-start.2
  65.3 8.9 %scatter.1.forcing_ref = f32[4,64,2048]{2,1,0:T(8,128)} custom-call(s32[32,128]{1,0:T(8,128)} %bitcast.7, f32[32,8,128]{2,1,0:T(8,128)} %get-tuple-element.30.terms_ref), custom_call_target="tpu_custom_call" | custom-call | tf_op jit(solution)/shard_map/scatter/pallas_call | solution.py:313
  74.2 0.0 collective-permute-done.low_ref
  74.2 0.0 collective-permute-done.1.high_ref
  74.2 0.0 copy-done
  74.2 0.0 copy-done.1
  74.2 0.0 copy-done.2
  74.2 47.0 %chain.1 = f32[1,4,64,2048]{3,2,1,0:T(8,128)S(1)} custom-call(f32[1,4,64,2048]{3,2,1,0:T(8,128)} %coeff_ref.3, bf16[1,64,2048]{2,1,0:T(8,128)(2,1)S(1)} %collective-permute-done.low_ref, bf16[1,64,2048]{2,1,0:T(8,128)(2,1)S(1)} %collective-permute-done.1.high_ref, bf16[2,64,2048]{2,1,0:T(8,128)(2,1)S(1)} %copy-done.1, bf16[2,64,2048]{2,1,0:T(8,128)(2,1)S(1)} %copy-done.2, ...), custom_call_target="tpu_custom_call" | custom-call | tf_op jit(solution)/shard_map/chain/pallas_call | solution.py:490
  121.2 1.3 %copy.11 = f32[1,4,64,2048]{3,2,1,0:T(8,128)} copy(f32[1,4,64,2048]{3,2,1,0:T(8,128)S(1)} %chain.1) | data formatting | bytes 4194304
Async XLA Ops:
  16.2 57.9 %collective-permute-start = (bf16[1,64,2048]{2,1,0:T(8,128)(2,1)}, bf16[1,64,2048]{2,1,0:T(8,128)(2,1)S(1)}, u32[]{:S(2)}, u32[]{:S(2)}) collective-permute-start(bf16[1,64,2048]{2,1,0:T(8,128)(2,1)} %get-tuple-element.21), channel_id=1, source_target_pairs={{0,1},{1,2},{2,3},{3,4},{4,5},{5,6},{6,7},{8,9},{9,10},{10,11},{11... | collective-permute-start | bytes 786440 | tf_op jit(solution)/shard_map/ppermute | solution.py:537
  19.6 54.6 %collective-permute-start.1 = (bf16[1,64,2048]{2,1,0:T(8,128)(2,1)}, bf16[1,64,2048]{2,1,0:T(8,128)(2,1)S(1)}, u32[]{:S(2)}, u32[]{:S(2)}) collective-permute-start(bf16[1,64,2048]{2,1,0:T(8,128)(2,1)} %get-tuple-element.22), channel_id=1, source_target_pairs={{1,0},{2,1},{3,2},{4,3},{5,4},{6,5},{7,6},{9,8},{10,9},{11,10},{12... | collective-permute-start | bytes 786440 | tf_op jit(solution)/shard_map/ppermute | solution.py:538
  50.4 23.8 %copy-start = (bf16[4,64,2048]{2,1,0:T(8,128)(2,1)S(1)}, bf16[4,64,2048]{2,1,0:T(8,128)(2,1)}, u32[]{:S(2)}) copy-start(bf16[4,64,2048]{2,1,0:T(8,128)(2,1)} %end_ref.3) | copy-start | bytes 3145732
  50.4 23.8 %copy-start.1 = (bf16[2,64,2048]{2,1,0:T(8,128)(2,1)S(1)}, bf16[2,64,2048]{2,1,0:T(8,128)(2,1)}, u32[]{:S(2)}) copy-start(bf16[2,64,2048]{2,1,0:T(8,128)(2,1)} %get-tuple-element.25.last_low_ref) | copy-start | bytes 1572868
  65.2 8.9 %copy-start.2 = (bf16[2,64,2048]{2,1,0:T(8,128)(2,1)S(1)}, bf16[2,64,2048]{2,1,0:T(8,128)(2,1)}, u32[]{:S(2)}) copy-start(bf16[2,64,2048]{2,1,0:T(8,128)(2,1)} %get-tuple-element.29.last_high_ref) | copy-start | bytes 1572868
where the time goes:
time: 123 us; the launch traced here: 122 us
  Pallas kernels  114 us (93%)
  starting transfers between devices  6.73 us (5%)
  local copies, waits for them, and re-layouts  1.33 us (1%)
    pallas_call x1, Pallas kernels, chain(): pl.pallas_call(functools.partial(chain_kernel, lax.axis_size('tm'), lax.a...  47 us
    pallas_call x2, Pallas kernels, exchange(): pl.pallas_call(functools.partial(exchange_kernel, count, lat, shift), out...  25.8 us
    pallas_call x1, Pallas kernels, exchange(): pl.pallas_call(functools.partial(exchange_kernel, count, lat, 0), out_sha...  9.73 us
    pallas_call x1, Pallas kernels, scatter(): pl.pallas_call(functools.partial(scatter_kernel, slots), out_shape=jax.Sh...  8.9 us
    pallas_call x1, Pallas kernels, gather(): pl.pallas_call(functools.partial(gather_kernel, slots), out_shape=jax.Sha...  8.66 us
    pallas_call x1, Pallas kernels, block_terms(): pl.pallas_call(blocks_kernel, out_shape=jax.ShapeDtypeStruct(states.shape...  7.76 us
    pallas_call x1, Pallas kernels, last_edges(): pl.pallas_call(last_edges_kernel, out_shape=(edge, edge, single, single),...  3.82 us
    ppermute x1, starting transfers between devices, per_device(): high = lax.ppermute(edges[0], 'lat', downward)  3.4 us
  transfers between devices with their start and end apart: 2, of which 0 were waited for; matrix products, arithmetic and copies ran while one was open for 0% of the time, Pallas kernels for 42%

commit v1 on v0

v1 whole, which is shorter than its diff:
```python
import functools

import jax
import jax.numpy as jnp
from jax import lax
from jax.experimental import pallas as pl
from jax.experimental.pallas import tpu as pltpu
from jax.sharding import PartitionSpec as P

TW = 2
SUB = 2
LANES = 128
PAD = 8
CHUNK = 8
MESH = pl.DeviceIdType.MESH
VMEM = pl.BlockSpec(memory_space=pltpu.VMEM)


def split(x):
    top = x.astype(jnp.bfloat16)
    return top, (x - top.astype(jnp.float32)).astype(jnp.bfloat16)


def dot(a, b):
    return jnp.dot(a, b, preferred_element_type=jnp.float32)


def iota(shape, axis):
    return lax.broadcasted_iota(jnp.int32, shape, axis)


def ones_where(mask):
    return jnp.where(mask, 1.0, 0.0)


def observe_kernel(
    lats, count, slots,
    owner_ref, tile_ref, value_ref, weight_ref, valid_ref, traj_hbm, coeff_hbm, end_hbm, jac_hbm,
    forcing_ref, low_ref, high_ref, last_low_ref, last_high_ref,
    traj, coeff, end, jac, jac_t, fields, chosen, place, place_t,
    ids_out, ids_in, state_out, state_in, term_out, term_in, state_rows, resid_rows, terms,
    first_row, final_row, edge_low, edge_high,
    load_sem, ids_send, ids_recv, state_send, state_recv, term_send, term_recv, row_send, row_recv, edge_send, edge_recv,
):
    section, band = lax.axis_index("tm"), lax.axis_index("lat")
    me = section * lats + band
    rows, levels, nlon = forcing_ref.shape
    blocks = owner_ref.shape[1]
    total = count * PAD
    columns = nlon // LANES
    per_column = LANES // TW
    tile_len = levels * TW

    loads = [
        pltpu.make_async_copy(src, dst, load_sem.at[i])
        for i, (src, dst) in enumerate(
            ((traj_hbm.at[0], traj), (coeff_hbm.at[0], coeff), (end_hbm, end), (jac_hbm, jac))
        )
    ]
    for load in loads:
        load.start()

    barrier = pltpu.get_barrier_semaphore()

    def peer(j):
        to = lax.rem(me + j, count)
        return to, (to // lats, lax.rem(to, lats))

    def greet(j, carry):
        pl.semaphore_signal(barrier, inc=1, device_id=peer(j)[1], device_id_type=MESH)
        return carry

    lax.fori_loop(1, count, greet, 0)

    def swap(out, into, send, recv):
        def outgoing(j):
            to, where = peer(j)
            return pltpu.make_async_remote_copy(
                src_ref=out.at[to], dst_ref=into.at[me], send_sem=send.at[j], recv_sem=recv.at[j],
                device_id=where, device_id_type=MESH,
            )

        def incoming(j):
            source, where = peer(count - j)
            return pltpu.make_async_remote_copy(
                src_ref=out.at[source], dst_ref=into.at[source], send_sem=send.at[j], recv_sem=recv.at[j],
                device_id=where, device_id_type=MESH,
            )

        def launch(j, carry):
            outgoing(j).start()
            return carry

        def land(j, carry):
            incoming(j).wait_recv()
            return carry

        def drain(j, carry):
            outgoing(j).wait_send()
            return carry

        def begin():
            lax.fori_loop(1, count, launch, 0)
            into[me] = out[me]

        return begin, lambda: lax.fori_loop(1, count, land, 0), lambda: lax.fori_loop(1, count, drain, 0)

    ids_begin, ids_land, ids_drain = swap(ids_out, ids_in, ids_send, ids_recv)
    state_begin, state_land, state_drain = swap(state_out, state_in, state_send, state_recv)
    term_begin, term_land, term_drain = swap(term_out, term_in, term_send, term_recv)

    owner = owner_ref[...]
    mine = owner == iota((count, blocks), 0)
    before = ones_where(iota((blocks, blocks), 0) < iota((blocks, blocks), 1)).astype(jnp.bfloat16)
    rank = dot(ones_where(mine).astype(jnp.bfloat16), before)
    target = jnp.where(mine, iota((count, blocks), 0).astype(jnp.float32) * PAD + rank, 0.0)
    slot = jnp.sum(target, axis=0, keepdims=True)
    tile = tile_ref[...]
    column = (tile // per_column + 1).astype(jnp.float32)
    inside = lax.rem(tile, per_column).astype(jnp.float32)
    lane = iota((count, LANES), 1)
    packed = jnp.zeros((count, LANES), jnp.float32)
    for s in range(slots):
        here = mine & (rank == float(s))
        for at, what in ((s, column), (PAD + s, inside)):
            found = jnp.sum(jnp.where(here, what, 0.0), axis=1, keepdims=True)
            packed = jnp.where(lane == at, found, packed)
    for d in range(count):
        ids_out[d] = packed[d : d + 1]
    pl.semaphore_wait(barrier, count - 1)
    ids_begin()

    holds = ones_where(iota((total, blocks), 0).astype(jnp.float32) == slot)
    place[...] = holds.astype(jnp.bfloat16)
    place_t[...] = holds.T.astype(jnp.bfloat16)

    for load in loads[:3]:
        load.wait()
    first_row[0] = coeff[0].astype(jnp.bfloat16)
    final_row[0] = coeff[rows - 1].astype(jnp.bfloat16)
    has_low, has_high = band > 0, band < lats - 1
    is_last = section == count // lats - 1

    def beside(src, dst, i, send, recv, shift):
        return pltpu.make_async_remote_copy(
            src_ref=src, dst_ref=dst, send_sem=send.at[i], recv_sem=recv.at[i],
            device_id=(section, band + shift), device_id_type=MESH,
        )

    def row_down():
        return beside(first_row, high_ref, 0, row_send, row_recv, -1)

    def row_up():
        return beside(final_row, low_ref, 1, row_send, row_recv, 1)

    def edge_down():
        return beside(edge_low, last_high_ref, 0, edge_send, edge_recv, -1)

    def edge_up():
        return beside(edge_high, last_low_ref, 1, edge_send, edge_recv, 1)

    @pl.when(has_low)
    def _():
        row_down().start()

    @pl.when(has_high)
    def _():
        row_up().start()

    @pl.when(jnp.logical_not(has_low))
    def _():
        low_ref[...] = jnp.zeros_like(low_ref)

    @pl.when(jnp.logical_not(has_high))
    def _():
        high_ref[...] = jnp.zeros_like(high_ref)

    @pl.when(jnp.logical_not(has_low & is_last))
    def _():
        last_low_ref[...] = jnp.zeros_like(last_low_ref)

    @pl.when(jnp.logical_not(has_high & is_last))
    def _():
        last_high_ref[...] = jnp.zeros_like(last_high_ref)

    even = lax.rem(iota((levels, nlon), 1), TW)

    def field(r, carry):
        values = traj[r]
        top = values.astype(jnp.bfloat16).astype(jnp.float32)
        parts = [jnp.where(even == p, x, 0.0) for x in (top, values - top) for p in range(TW)]
        fields[r] = jnp.concatenate(parts, axis=0).T.astype(jnp.bfloat16)
        return carry

    lax.fori_loop(0, rows, field, 0)

    ids_land()
    ids = jnp.concatenate([ids_in[d] for d in range(count)], axis=0).astype(jnp.bfloat16)
    source = ones_where(iota((total, count), 0) // PAD == iota((total, count), 1)).astype(jnp.bfloat16)
    spread = dot(source, ids)
    nth = lax.rem(iota((total, LANES), 0), PAD)
    lanes = iota((total, LANES), 1)
    which = jnp.sum(jnp.where(lanes == nth, spread, 0.0), axis=1, keepdims=True)
    inner = jnp.sum(jnp.where(lanes == nth + PAD, spread, 0.0), axis=1, keepdims=True)
    which = jnp.broadcast_to(which, (total, LANES)).astype(jnp.bfloat16)
    pair = ones_where((lanes // TW).astype(jnp.float32) == inner).astype(jnp.bfloat16)
    nothing = jnp.zeros_like(pair)
    gathered = jnp.zeros((total, 2 * tile_len), jnp.float32)
    for r in range(rows):
        for c in range(columns):
            chosen[r, :, c * LANES : (c + 1) * LANES] = jnp.where(
                which == jnp.bfloat16(r * columns + c + 1), pair, nothing
            )
        gathered = gathered + dot(chosen[r], fields[r])
    states = gathered[:, :tile_len] + gathered[:, tile_len:]
    state_out[...] = states.reshape(count, PAD, tile_len)
    state_begin()

    loads[3].wait()

    def turn(k, carry):
        jac_t[k] = jac[k].astype(jnp.float32).T.astype(jnp.bfloat16)
        return carry

    lax.fori_loop(0, blocks, turn, 0, unroll=4)

    @pl.when(is_last)
    def _():
        def one(c, carry):
            span = pl.ds(pl.multiple_of(c * 16, 16), 16)

            def weigh(r):
                return coeff[r, span, :] * end[r, span, :].astype(jnp.float32)

            for r, near, ref in ((0, 1, edge_low), (rows - 1, rows - 2, edge_high)):
                mid = weigh(r)
                value = end[r, span, :].astype(jnp.float32) + weigh(near)
                value = value + pltpu.roll(mid, 1, 1) + pltpu.roll(mid, nlon - 1, 1) - 4.0 * mid
                ref[0, span, :] = mid.astype(jnp.bfloat16)
                ref[1, span, :] = (coeff[r, span, :] * value).astype(jnp.bfloat16)
            return carry

        lax.fori_loop(0, levels // 16, one, 0)

    @pl.when(has_low & is_last)
    def _():
        edge_down().start()

    @pl.when(has_high & is_last)
    def _():
        edge_up().start()

    order = iota((tile_len, tile_len), 0)
    other = iota((tile_len, tile_len), 1)

    def by_part(a, b):
        same = (a // TW == lax.rem(b, levels)) & (lax.rem(a, TW) == b // levels)
        return ones_where(same).astype(jnp.bfloat16)

    to_parts, from_parts = by_part(order, other), by_part(other, order)

    state_land()
    top, rest = split(state_in[...].reshape(total, tile_len))
    own = dot(place_t[...], jnp.concatenate([top, rest], axis=1)).astype(jnp.bfloat16)
    top, rest = dot(own[:, :tile_len], from_parts), dot(own[:, tile_len:], from_parts)
    groups = blocks // PAD
    for g in range(groups):
        span = slice(g * PAD, (g + 1) * PAD)
        state_rows[g] = jnp.concatenate([top[span], rest[span]], axis=0).astype(jnp.bfloat16)
    among = lax.rem(iota((2 * PAD, tile_len), 0), PAD)

    def product(both, mats, g):
        picked = jnp.zeros((2 * PAD, tile_len), jnp.float32)
        for i in range(PAD):
            picked = jnp.where(among == i, dot(both, mats[g * PAD + i]), picked)
        return picked[:PAD] + picked[PAD:]

    for g in range(groups):
        here = slice(g * PAD, (g + 1) * PAD)
        pred = product(state_rows[g], jac_t, g)
        weight = weight_ref[here, :] * valid_ref[here, :].astype(jnp.float32)
        resid = weight * (value_ref[here, :] - pred)
        top = resid.astype(jnp.bfloat16).astype(jnp.float32)
        resid_rows[g] = jnp.concatenate([top, resid - top], axis=0).astype(jnp.bfloat16)
    for g in range(groups):
        terms[g * PAD : (g + 1) * PAD, :] = product(resid_rows[g], jac, g)
    top, rest = split(terms[...])
    top, rest = dot(top, to_parts).astype(jnp.bfloat16), dot(rest, to_parts).astype(jnp.bfloat16)
    sent = dot(place[...], top) + dot(place[...], rest)
    term_out[...] = sent.reshape(count, PAD, tile_len)
    term_begin()
    ids_drain()
    state_drain()

    term_land()
    got = term_in[...].reshape(total, tile_len).T
    top, rest = split(got)
    parity = lax.rem(iota((levels, nlon), 1), TW)
    for r in range(rows):
        both = dot(top, chosen[r]) + dot(rest, chosen[r])
        forcing_ref[r] = jnp.where(parity == 0, both[:levels], both[levels:])
    term_drain()

    for cond, copy in (
        (has_low, row_down), (has_high, row_up), (has_low & is_last, edge_down), (has_high & is_last, edge_up)
    ):
        @pl.when(cond)
        def _(copy=copy):
            copy().wait_send()

    for cond, copy in (
        (has_high, row_down), (has_low, row_up), (has_high & is_last, edge_down), (has_low & is_last, edge_up)
    ):
        @pl.when(cond)
        def _(copy=copy):
            copy().wait_recv()


def observe(owner, tile, value, weight, valid, traj, coeff, end, jac, slots):
    lats = lax.axis_size("lat")
    count = lax.axis_size("tm") * lats
    _, rows, levels, nlon = traj.shape
    blocks = owner.shape[1]
    tile_len = levels * TW
    total = count * PAD
    bf16, f32 = jnp.bfloat16, jnp.float32
    edge = jax.ShapeDtypeStruct((SUB, levels, nlon), bf16)
    single = jax.ShapeDtypeStruct((1, levels, nlon), bf16)
    lists = pltpu.VMEM((count, 1, LANES), f32)
    parcels = pltpu.VMEM((count, PAD, tile_len), f32)
    stacked = pltpu.VMEM((blocks // PAD, 2 * PAD, tile_len), bf16)
    anywhere = pl.BlockSpec(memory_space=pl.ANY)
    dma = pltpu.SemaphoreType.DMA
    return pl.pallas_call(
        functools.partial(observe_kernel, lats, count, slots),
        out_shape=(jax.ShapeDtypeStruct((rows, levels, nlon), f32), single, single, edge, edge),
        in_specs=[VMEM] * 5 + [anywhere] * 4,
        out_specs=(VMEM,) * 5,
        scratch_shapes=[
            pltpu.VMEM((rows, levels, nlon), f32),
            pltpu.VMEM((rows, levels, nlon), f32),
            pltpu.VMEM((rows, levels, nlon), bf16),
            pltpu.VMEM(jac.shape, bf16),
            pltpu.VMEM(jac.shape, bf16),
            pltpu.VMEM((rows, nlon, 2 * tile_len), bf16),
            pltpu.VMEM((rows, total, nlon), bf16),
            pltpu.VMEM((total, blocks), bf16),
            pltpu.VMEM((blocks, total), bf16),
            lists, lists, parcels, parcels, parcels, parcels, stacked, stacked,
            pltpu.VMEM((blocks, tile_len), f32),
            pltpu.VMEM((1, levels, nlon), bf16),
            pltpu.VMEM((1, levels, nlon), bf16),
            pltpu.VMEM((SUB, levels, nlon), bf16),
            pltpu.VMEM((SUB, levels, nlon), bf16),
            dma((4,)),
        ]
        + [dma((count,))] * 6
        + [dma((2,))] * 4,
        compiler_params=pltpu.CompilerParams(
            collective_id=1, has_side_effects=True, vmem_limit_bytes=60 * 1024 * 1024
        ),
        name="observe",
    )(owner, tile, value, weight, valid, traj, coeff, end, jac)


def chain_kernel(
    sections, lats, coeff_ref, low_ref, high_ref, last_low_ref, last_high_ref, end_ref, forcing_ref, out_ref,
    main, low, high, edge_low, edge_high, ahead, weighted, partial, second,
    main_send, main_recv, down_send, up_send, low_recv, high_recv,
):
    section, band = lax.axis_index("tm"), lax.axis_index("lat")
    rows, levels, nlon = end_ref.shape
    chunks = levels // CHUNK
    is_last = section == sections - 1
    has_before, has_low, has_high = section > 0, band > 0, band < lats - 1

    sends_low, sends_high = has_low & jnp.logical_not(is_last), has_high & jnp.logical_not(is_last)

    barrier = pltpu.get_barrier_semaphore()
    sides = (
        (jnp.logical_not(is_last), section + 1, band),
        (has_before, section - 1, band),
        (has_low, section, band - 1),
        (has_high, section, band + 1),
    )
    for there, tm, lat in sides:
        @pl.when(there)
        def _(tm=tm, lat=lat):
            pl.semaphore_signal(barrier, inc=1, device_id=(tm, lat), device_id_type=MESH)
    pl.semaphore_wait(barrier, sum(there.astype(jnp.int32) for there, _, _ in sides))

    def remote(src, dst, send, recv, tm, lat):
        return pltpu.make_async_remote_copy(
            src_ref=src, dst_ref=dst, send_sem=send, recv_sem=recv, device_id=(tm, lat), device_id_type=MESH
        )

    def local_main(c):
        return pltpu.make_async_copy(
            end_ref.at[:, pl.ds(pl.multiple_of(c * CHUNK, CHUNK), CHUNK), :], main.at[c], main_recv.at[c]
        )

    def handed(c):
        return remote(ahead.at[c], main.at[c], main_send.at[c], main_recv.at[c], section - 1, band)

    def downward(c):
        return remote(edge_low.at[c], high.at[c], down_send.at[c], high_recv.at[c], section, band - 1)

    def upward(c):
        return remote(edge_high.at[c], low.at[c], up_send.at[c], low_recv.at[c], section, band + 1)

    @pl.when(jnp.logical_not(has_low))
    def _():
        low[...] = jnp.zeros_like(low)

    @pl.when(jnp.logical_not(has_high))
    def _():
        high[...] = jnp.zeros_like(high)

    @pl.when(is_last)
    def _():
        for c in range(chunks):
            local_main(c).start()
            low[c] = last_low_ref[:, c * CHUNK : (c + 1) * CHUNK, :]
            high[c] = last_high_ref[:, c * CHUNK : (c + 1) * CHUNK, :]

    def levels_of(c):
        return pl.ds(pl.multiple_of(c * CHUNK, CHUNK), CHUNK)

    def along(mid):
        return pltpu.roll(mid, 1, 1) + pltpu.roll(mid, nlon - 1, 1) - 4.0 * mid

    def begin(c):
        @pl.when(is_last)
        def _():
            local_main(c).wait()

        @pl.when(jnp.logical_not(is_last))
        def _():
            handed(c).wait_recv()

        span = levels_of(c)
        for r in range(rows):
            weighted[c, r] = coeff_ref[0, r, span, :] * main[c, r].astype(jnp.float32)
        for r in range(rows):
            mid = weighted[c, r]
            value = main[c, r].astype(jnp.float32) + along(mid)
            if r > 0:
                value = value + weighted[c, r - 1]
            if r < rows - 1:
                value = value + weighted[c, r + 1]
            partial[c, r] = value
            if r == 0:
                edge_low[c, 0] = mid.astype(jnp.bfloat16)
                edge_low[c, 1] = (coeff_ref[0, r, span, :] * value).astype(jnp.bfloat16)
            if r == rows - 1:
                edge_high[c, 0] = mid.astype(jnp.bfloat16)
                edge_high[c, 1] = (coeff_ref[0, r, span, :] * value).astype(jnp.bfloat16)

        @pl.when(sends_low)
        def _():
            downward(c).start()

        @pl.when(sends_high)
        def _():
            upward(c).start()

    def complete(c):
        span = levels_of(c)
        end = rows - 1
        partial[c, 0] = partial[c, 0] + low[c, 0].astype(jnp.float32)
        partial[c, end] = partial[c, end] + high[c, 0].astype(jnp.float32)
        second[0] = low[c, 1].astype(jnp.float32) + low_ref[0, span, :].astype(jnp.float32) * weighted[c, 0]
        second[rows + 1] = high[c, 1].astype(jnp.float32) + high_ref[0, span, :].astype(jnp.float32) * weighted[c, end]
        for r in range(rows):
            second[r + 1] = coeff_ref[0, r, span, :] * partial[c, r]
        for r in range(rows):
            value = partial[c, r] + second[r] + second[r + 2] + along(second[r + 1]) + forcing_ref[r, span, :]
            out_ref[0, r, span, :] = value
            ahead[c, r] = value.astype(jnp.bfloat16)

    look = jnp.where(section == sections - 2, min(4, chunks), min(2, chunks))

    def open_one(c, carry):
        begin(c)
        return carry

    lax.fori_loop(0, look, open_one, 0)

    def step(c, carry):
        @pl.when(c + look < chunks)
        def _():
            begin(c + look)

        @pl.when(sends_low)
        def _():
            upward(c).wait_recv()

        @pl.when(sends_high)
        def _():
            downward(c).wait_recv()

        complete(c)

        @pl.when(has_before)
        def _():
            handed(c).start()

        return carry

    lax.fori_loop(0, chunks, step, 0)

    def finish(c, carry):
        @pl.when(sends_low)
        def _():
            downward(c).wait_send()

        @pl.when(sends_high)
        def _():
            upward(c).wait_send()

        @pl.when(has_before)
        def _():
            handed(c).wait_send()

        return carry

    lax.fori_loop(0, chunks, finish, 0)


def chain(coeff, low, high, last_low, last_high, end, forcing):
    rows, levels, nlon = end.shape
    chunks = levels // CHUNK
    part = lambda n, kind: pltpu.VMEM((chunks, n, CHUNK, nlon), kind)
    return pl.pallas_call(
        functools.partial(chain_kernel, lax.axis_size("tm"), lax.axis_size("lat")),
        out_shape=jax.ShapeDtypeStruct(coeff.shape, jnp.float32),
        in_specs=[VMEM] * 7,
        out_specs=VMEM,
        scratch_shapes=[
            part(rows, jnp.bfloat16),
            part(SUB, jnp.bfloat16),
            part(SUB, jnp.bfloat16),
            part(SUB, jnp.bfloat16),
            part(SUB, jnp.bfloat16),
            part(rows, jnp.bfloat16),
            part(rows, jnp.float32),
            part(rows, jnp.float32),
            pltpu.VMEM((rows + 2, CHUNK, nlon), jnp.float32),
        ]
        + [pltpu.SemaphoreType.DMA((chunks,))] * 6,
        compiler_params=pltpu.CompilerParams(
            collective_id=9, has_side_effects=True, vmem_limit_bytes=48 * 1024 * 1024
        ),
        name="chain",
    )(coeff, low, high, last_low, last_high, end, forcing)


def per_device(
    trajectory,
    diffusivity,
    adjoint_end,
    obs_jac,
    obs_value,
    obs_weight,
    obs_valid,
    obs_owner,
    obs_tile,
):
    devices = lax.axis_size("tm") * lax.axis_size("lat")
    blocks = obs_owner.shape[0]
    slots = max(2, 2 * blocks // devices)
    forcing, low, high, last_low, last_high = observe(
        obs_owner[:, 0][None, :], obs_tile[None, :], obs_value, obs_weight, obs_valid,
        trajectory, diffusivity, adjoint_end, obs_jac, slots,
    )
    return chain(diffusivity, low, high, last_low, last_high, adjoint_end, forcing)


def solution(mesh):
    in_specs = (
        P("tm", "lat", None, None),
        P("tm", "lat", None, None),
        P("lat", None, None),
        P(("tm", "lat"), None, None),
        P(("tm", "lat"), None),
        P(("tm", "lat"), None),
        P(("tm", "lat"), None),
        P(("tm", "lat"), None),
        P(("tm", "lat")),
    )
    out_specs = P("tm", "lat", None, None)
    return jax.shard_map(
        per_device, mesh=mesh, in_specs=in_specs, out_specs=out_specs, check_vma=False
    )
```

time: 123 us -> 88.8 us (0.72)
  Pallas kernels: 114 us -> 83.2 us
  starting transfers between devices: 6.73 us -> 0 us
  local copies, waits for them, and re-layouts: 1.33 us -> 5.3 us
    pallas_call x8 -> x1, Pallas kernels: 67.4 us -> 40.2 us  [observe(): pl.pallas_call(functools.partial(observe_kernel, lats, count, slots), out...]
    ppermute x2 -> x0, starting transfers between devices: 6.73 us -> none  [the longest x1 3.4 us: per_device(): high = lax.ppermute(edges[0], 'lat', downward)]
    pallas_call x1, Pallas kernels: 47 us -> 43 us  [chain(): pl.pallas_call(functools.partial(chain_kernel, lax.axis_size('tm'), lax.a...]
    unnamed x7 -> x11, local copies, waits for them, and re-layouts: 1.33 us -> 5.3 us
  transfers between devices with their start and end apart: 2 -> 0, of which waited for: 0 -> 0; matrix products, arithmetic and copies ran while one was open for 0% -> 0% of each run, Pallas kernels for 42% -> 0%
where the time goes in v1:
time: 88.8 us; the launch traced here: 88.5 us
  Pallas kernels  83.2 us (94%)
  local copies, waits for them, and re-layouts  5.3 us (6%)
    pallas_call x1, Pallas kernels, chain(): pl.pallas_call(functools.partial(chain_kernel, lax.axis_size('tm'), lax.a...  43 us
    pallas_call x1, Pallas kernels, observe(): pl.pallas_call(functools.partial(observe_kernel, lats, count, slots), out...  40.2 us
    unnamed x11, local copies, waits for them, and re-layouts  5.3 us

profile of v1, /device:TPU:8, one launch (start us, length us, event | category | flops | bytes accessed | tf_op | source)
XLA Modules:
  0.0 88.5 jit_solution(2975052031712361788)
XLA Ops:
  0.0 0.0 copy-start
  0.0 40.2 %observe.1 = (f32[4,64,2048]{2,1,0:T(8,128)}, bf16[1,64,2048]{2,1,0:T(8,128)(2,1)}, bf16[1,64,2048]{2,1,0:T(8,128)(2,1)}, bf16[2,64,2048]{2,1,0:T(8,128)(2,1)}, bf16[2,64,2048]{2,1,0:T(8,128)(2,1)}) custom-call(s32[1,96]{1,0:T(1,128)} %bitcast.2, s32[1,96]{1,0:T(1,128)} %bitcast.3, f32[96,128]{1,0:T(8,128)} %value_ref.1, f32[96,128]{1,0:T(8,128)} %weight_ref.1, ...), custom_call_target="tpu_custom_call" | custom-call | tf_op jit(solution)/shard_map/observe/pallas_call | solution.py:334
  40.2 0.0 copy-done
  40.2 0.0 copy-start.1
  40.2 1.0 %copy-done.1 = bf16[2,64,2048]{2,1,0:T(8,128)(2,1)S(1)} copy-done((bf16[2,64,2048]{2,1,0:T(8,128)(2,1)S(1)}, bf16[2,64,2048]{2,1,0:T(8,128)(2,1)}, u32[]{:S(2)}) %copy-start.1) | copy-done | bytes 524312
  41.3 0.0 copy-start.2
  41.3 1.0 %copy-done.2 = bf16[2,64,2048]{2,1,0:T(8,128)(2,1)S(1)} copy-done((bf16[2,64,2048]{2,1,0:T(8,128)(2,1)S(1)}, bf16[2,64,2048]{2,1,0:T(8,128)(2,1)}, u32[]{:S(2)}) %copy-start.2) | copy-done | bytes 524312
  42.3 0.0 copy-start.3
  42.3 0.9 %copy-done.3 = bf16[1,64,2048]{2,1,0:T(8,128)(2,1)S(1)} copy-done((bf16[1,64,2048]{2,1,0:T(8,128)(2,1)S(1)}, bf16[1,64,2048]{2,1,0:T(8,128)(2,1)}, u32[]{:S(2)}) %copy-start.3) | copy-done | bytes 262168
  43.3 0.0 copy-start.4
  43.3 0.9 %copy-done.4 = bf16[1,64,2048]{2,1,0:T(8,128)(2,1)S(1)} copy-done((bf16[1,64,2048]{2,1,0:T(8,128)(2,1)S(1)}, bf16[1,64,2048]{2,1,0:T(8,128)(2,1)}, u32[]{:S(2)}) %copy-start.4) | copy-done | bytes 262168
  44.2 43.0 %chain.1 = f32[1,4,64,2048]{3,2,1,0:T(8,128)S(1)} custom-call(f32[1,4,64,2048]{3,2,1,0:T(8,128)} %coeff_ref.1, bf16[1,64,2048]{2,1,0:T(8,128)(2,1)S(1)} %copy-done.3, bf16[1,64,2048]{2,1,0:T(8,128)(2,1)S(1)} %copy-done.4, bf16[2,64,2048]{2,1,0:T(8,128)(2,1)S(1)} %copy-done.1, bf16[2,64,2048]{2,1,0:T(8,128)(2,1)S(1)} %copy-done.2, ...), custom_call_target="tpu_custom_call" | custom-call | tf_op jit(solution)/shard_map/chain/pallas_call | solution.py:534
  87.2 1.3 %copy.11 = f32[1,4,64,2048]{3,2,1,0:T(8,128)} copy(f32[1,4,64,2048]{3,2,1,0:T(8,128)S(1)} %chain.1) | data formatting | bytes 4194304
Async XLA Ops:
  0.0 40.2 %copy-start = (bf16[4,64,2048]{2,1,0:T(8,128)(2,1)S(1)}, bf16[4,64,2048]{2,1,0:T(8,128)(2,1)}, u32[]{:S(2)}) copy-start(bf16[4,64,2048]{2,1,0:T(8,128)(2,1)} %end_ref.1) | copy-start | bytes 3145732
  40.2 1.0 %copy-start.1 = (bf16[2,64,2048]{2,1,0:T(8,128)(2,1)S(1)}, bf16[2,64,2048]{2,1,0:T(8,128)(2,1)}, u32[]{:S(2)}) copy-start(bf16[2,64,2048]{2,1,0:T(8,128)(2,1)} %get-tuple-element.12.last_low_ref) | copy-start | bytes 1572868
  41.3 1.0 %copy-start.2 = (bf16[2,64,2048]{2,1,0:T(8,128)(2,1)S(1)}, bf16[2,64,2048]{2,1,0:T(8,128)(2,1)}, u32[]{:S(2)}) copy-start(bf16[2,64,2048]{2,1,0:T(8,128)(2,1)} %get-tuple-element.13.last_high_ref) | copy-start | bytes 1572868
  42.3 0.9 %copy-start.3 = (bf16[1,64,2048]{2,1,0:T(8,128)(2,1)S(1)}, bf16[1,64,2048]{2,1,0:T(8,128)(2,1)}, u32[]{:S(2)}) copy-start(bf16[1,64,2048]{2,1,0:T(8,128)(2,1)} %get-tuple-element.10.low_ref) | copy-start | bytes 786436
  43.3 0.9 %copy-start.4 = (bf16[1,64,2048]{2,1,0:T(8,128)(2,1)S(1)}, bf16[1,64,2048]{2,1,0:T(8,128)(2,1)}, u32[]{:S(2)}) copy-start(bf16[1,64,2048]{2,1,0:T(8,128)(2,1)} %get-tuple-element.11.high_ref) | copy-start | bytes 786436

commit v2 on v1

v2 whole, which is shorter than its diff:
```python
import functools

import jax
import jax.numpy as jnp
from jax import lax
from jax.experimental import pallas as pl
from jax.experimental.pallas import tpu as pltpu
from jax.sharding import PartitionSpec as P

TW = 2
SUB = 2
LANES = 128
PAD = 8
CHUNK = 8
SCALE = 2.0**17
MESH = pl.DeviceIdType.MESH
VMEM = pl.BlockSpec(memory_space=pltpu.VMEM)


def split(x):
    top = x.astype(jnp.bfloat16)
    return top, (x - top.astype(jnp.float32)).astype(jnp.bfloat16)


def dot(a, b):
    return jnp.dot(a, b, preferred_element_type=jnp.float32)


def iota(shape, axis):
    return lax.broadcasted_iota(jnp.int32, shape, axis)


def ones_where(mask):
    return jnp.where(mask, 1.0, 0.0)


def sweep_kernel(
    lats, sections, slots,
    owner_hbm, tile_hbm, value_hbm, weight_hbm, valid_hbm, traj_hbm, coeff_hbm, end_hbm, jac_hbm,
    out_ref,
    owner_ref, tile_ref, value_ref, weight_ref, valid_ref, traj, coeff, jac, jac_t, fields, chosen, place, place_t, which, pair,
    ids_out, ids_in, state_out, state_in, term_out, term_in, state_rows, resid_rows, terms, terms_t,
    coded, kappa, kappa_low, kappa_high, main, forcing, weighted, partial, second, early,
    edge_low, edge_high, low, high,
    load_sem, end_sem, ids_send, ids_recv, state_send, state_recv, term_send, term_recv,
    kappa_send, kappa_recv, down_send, down_recv, up_send, up_recv,
    low_send, low_recv, high_send, high_recv, out_send, out_recv,
):
    section, band = lax.axis_index("tm"), lax.axis_index("lat")
    count = sections * lats
    me = section * lats + band
    rows, levels, nlon = coeff.shape
    blocks = owner_ref.shape[1]
    total = count * PAD
    columns = nlon // LANES
    per_column = LANES // TW
    tile_len = levels * TW
    part = levels // sections
    chunks = part // CHUNK
    width = part * TW
    has_low, has_high = band > 0, band < lats - 1
    last = sections - 1

    loads = [
        pltpu.make_async_copy(src, dst, load_sem.at[i])
        for i, (src, dst) in enumerate(
            (
                (owner_hbm, owner_ref), (tile_hbm, tile_ref), (coeff_hbm.at[0], coeff), (traj_hbm.at[0], traj),
                (jac_hbm, jac), (value_hbm, value_ref), (weight_hbm, weight_ref), (valid_hbm, valid_ref),
            )
        )
    ]
    for load in loads:
        load.start()

    def end_load(c):
        at = pl.multiple_of(section * part + c * CHUNK, CHUNK)
        return pltpu.make_async_copy(end_hbm.at[:, pl.ds(at, CHUNK), :], main.at[sections, c], end_sem.at[c])

    for c in range(chunks):
        end_load(c).start()

    barrier = pltpu.get_barrier_semaphore()

    def peer(j):
        to = lax.rem(me + j, count)
        return to, (to // lats, lax.rem(to, lats))

    def greet(j, carry):
        pl.semaphore_signal(barrier, inc=1, device_id=peer(j)[1], device_id_type=MESH)
        return carry

    lax.fori_loop(1, count, greet, 0)

    def remote(src, dst, send, recv, where):
        return pltpu.make_async_remote_copy(
            src_ref=src, dst_ref=dst, send_sem=send, recv_sem=recv, device_id=where, device_id_type=MESH
        )

    def swap(pick, into, send, recv):
        def outgoing(j):
            to, where = peer(j)
            return remote(pick(to), into.at[me], send.at[j], recv.at[j], where)

        def incoming(j):
            source, where = peer(count - j)
            return remote(pick(source), into.at[source], send.at[j], recv.at[j], where)

        def launch(j, carry):
            outgoing(j).start()
            return carry

        def land(j, carry):
            incoming(j).wait_recv()
            return carry

        def drain(j, carry):
            outgoing(j).wait_send()
            return carry

        def begin():
            lax.fori_loop(1, count, launch, 0)
            into[me] = pick(me)[...]

        return begin, lambda: lax.fori_loop(1, count, land, 0), lambda: lax.fori_loop(1, count, drain, 0)

    ids_begin, ids_land, ids_drain = swap(lambda d: ids_out.at[lax.rem(d, lats)], ids_in, ids_send, ids_recv)
    state_begin, state_land, state_drain = swap(lambda d: state_out.at[d], state_in, state_send, state_recv)
    term_begin, term_land, term_drain = swap(lambda d: term_out.at[d], term_in, term_send, term_recv)

    for load in loads[:2]:
        load.wait()
    owner = owner_ref[...]
    mine = owner == iota((count, blocks), 0)
    before = ones_where(iota((blocks, blocks), 0) < iota((blocks, blocks), 1)).astype(jnp.bfloat16)
    rank = dot(ones_where(mine).astype(jnp.bfloat16), before)
    target = jnp.where(mine, iota((count, blocks), 0).astype(jnp.float32) * PAD + rank, 0.0)
    slot = jnp.sum(target, axis=0, keepdims=True)
    tile = tile_ref[...]
    column = (tile // per_column + 1).astype(jnp.float32)
    inside = lax.rem(tile, per_column).astype(jnp.float32)
    lane = iota((count, LANES), 1)
    packed = jnp.zeros((count, LANES), jnp.float32)
    for s in range(slots):
        here = mine & (rank == float(s))
        for at, what in ((s, column), (PAD + s, inside)):
            found = jnp.sum(jnp.where(here, what, 0.0), axis=1, keepdims=True)
            packed = jnp.where(lane == at, found, packed)
    lists = packed[:lats]
    for s in range(1, sections):
        lists = lists + pltpu.roll(packed[s * lats : (s + 1) * lats], s * 2 * PAD, 1)
    for b in range(lats):
        ids_out[b] = lists[b : b + 1]
    pl.semaphore_wait(barrier, count - 1)
    ids_begin()

    def kappa_copy(j):
        to = lax.rem(section + j, sections)
        return remote(coded.at[to], kappa.at[section], kappa_send.at[j], kappa_recv.at[j], (to, band))

    def kappa_arrival(j):
        source = lax.rem(section + sections - j, sections)
        return remote(coded.at[source], kappa.at[source], kappa_send.at[j], kappa_recv.at[j], (source, band))

    def row_down(j):
        to = lax.rem(section + j, sections)
        return remote(coded.at[to, :, 0], kappa_high.at[section], down_send.at[j], down_recv.at[j], (to, band - 1))

    def row_up(j):
        to = lax.rem(section + j, sections)
        return remote(coded.at[to, :, rows - 1], kappa_low.at[section], up_send.at[j], up_recv.at[j], (to, band + 1))

    def from_high(j):
        source = lax.rem(section + sections - j, sections)
        return remote(coded.at[source, :, 0], kappa_high.at[source], down_send.at[j], down_recv.at[j], (source, band))

    def from_low(j):
        source = lax.rem(section + sections - j, sections)
        return remote(coded.at[source, :, 0], kappa_low.at[source], up_send.at[j], up_recv.at[j], (source, band))

    def share():
        for j in range(1, sections):
            kappa_copy(j).start()

        @pl.when(has_low)
        def _():
            for j in range(sections):
                row_down(j).start()

        @pl.when(has_high)
        def _():
            for j in range(sections):
                row_up(j).start()

    loads[2].wait()

    def encode(q, carry):
        for c in range(chunks):
            at = pl.multiple_of(q * part + c * CHUNK, CHUNK)
            for r in range(rows):
                scaled = coeff[r, pl.ds(at, CHUNK), :] * SCALE + 0.5
                coded[q, c, r] = scaled.astype(jnp.int32).astype(jnp.int16)
        return carry

    lax.fori_loop(0, sections, encode, 0)
    is_odd = lax.rem(section, 2) == lax.rem(last, 2)

    @pl.when(is_odd)
    def _():
        share()

    kappa[section] = coded[section]

    holds = ones_where(iota((total, blocks), 0).astype(jnp.float32) == slot)
    place[...] = holds.astype(jnp.bfloat16)
    place_t[...] = holds.T.astype(jnp.bfloat16)

    @pl.when(jnp.logical_not(has_low))
    def _():
        low[...] = jnp.zeros_like(low)
        kappa_low[...] = jnp.zeros_like(kappa_low)

    @pl.when(jnp.logical_not(has_high))
    def _():
        high[...] = jnp.zeros_like(high)
        kappa_high[...] = jnp.zeros_like(kappa_high)

    loads[3].wait()
    even = lax.rem(iota((levels, nlon), 1), TW)

    def field(r, carry):
        values = traj[r]
        top = values.astype(jnp.bfloat16).astype(jnp.float32)
        parts = [jnp.where(even == p, x, 0.0) for x in (top, values - top) for p in range(TW)]
        fields[r] = jnp.concatenate(parts, axis=0).T.astype(jnp.bfloat16)
        return carry

    lax.fori_loop(0, rows, field, 0)

    ids_land()
    ids = jnp.concatenate([ids_in[d] for d in range(count)], axis=0).astype(jnp.bfloat16)
    source = ones_where(iota((total, count), 0) // PAD == iota((total, count), 1)).astype(jnp.bfloat16)
    spread = dot(source, ids)
    nth = lax.rem(iota((total, LANES), 0), PAD)
    lanes = iota((total, LANES), 1)

    def listed(s):
        at = nth + s * 2 * PAD
        outer = jnp.sum(jnp.where(lanes == at, spread, 0.0), axis=1, keepdims=True)
        inner = jnp.sum(jnp.where(lanes == at + PAD, spread, 0.0), axis=1, keepdims=True)
        which[s] = jnp.broadcast_to(outer, (total, LANES)).astype(jnp.bfloat16)
        pair[s] = ones_where((lanes // TW).astype(jnp.float32) == inner).astype(jnp.bfloat16)

    nothing = jnp.zeros((total, LANES), jnp.bfloat16)

    def tiles(s, r, c):
        return jnp.where(which[s] == jnp.bfloat16(r * columns + c + 1), pair[s], nothing)

    listed(section)
    gathered = jnp.zeros((total, 2 * tile_len), jnp.float32)
    for r in range(rows):
        for c in range(columns):
            chosen[r, :, c * LANES : (c + 1) * LANES] = tiles(section, r, c)
        gathered = gathered + dot(chosen[r], fields[r])
    states = gathered[:, :tile_len] + gathered[:, tile_len:]
    state_out[...] = states.reshape(count, PAD, tile_len)
    state_begin()

    @pl.when(jnp.logical_not(is_odd))
    def _():
        share()

    for load in loads[4:]:
        load.wait()

    def turn(k, carry):
        jac_t[k] = jac[k].astype(jnp.float32).T.astype(jnp.bfloat16)
        return carry

    lax.fori_loop(0, blocks, turn, 0, unroll=4)

    def list_other(j, carry):
        listed(lax.rem(section + j, sections))
        return carry

    lax.fori_loop(1, sections, list_other, 0)

    def downward(s, c):
        return remote(edge_low.at[s, c], high.at[s, c], low_send.at[s, c], high_recv.at[s, c], (section, band - 1))

    def upward(s, c):
        return remote(edge_high.at[s, c], low.at[s, c], high_send.at[s, c], low_recv.at[s, c], (section, band + 1))

    def along(mid):
        return pltpu.roll(mid, 1, 1) + pltpu.roll(mid, nlon - 1, 1) - 4.0 * mid

    def decode(x):
        return x.astype(jnp.int32).astype(jnp.float32) * (1.0 / SCALE)

    def begin(s, c):
        for r in range(rows):
            weighted[c, r] = decode(kappa[s, c, r]) * main[s + 1, c, r].astype(jnp.float32)
        for r in range(rows):
            mid = weighted[c, r]
            value = main[s + 1, c, r].astype(jnp.float32) + along(mid)
            if r > 0:
                value = value + weighted[c, r - 1]
            if r < rows - 1:
                value = value + weighted[c, r + 1]
            partial[c, r] = value
            for at, ref in ((0, edge_low), (rows - 1, edge_high)):
                if r == at:
                    ref[s, c, 0] = mid.astype(jnp.bfloat16)
                    ref[s, c, 1] = (decode(kappa[s, c, r]) * value).astype(jnp.bfloat16)

        @pl.when(has_low)
        def _():
            downward(s, c).start()

        @pl.when(has_high)
        def _():
            upward(s, c).start()

    def complete(s, c, store):
        @pl.when(has_low)
        def _():
            upward(s, c).wait_recv()

        @pl.when(has_high)
        def _():
            downward(s, c).wait_recv()

        end = rows - 1
        partial[c, 0] = partial[c, 0] + low[s, c, 0].astype(jnp.float32)
        partial[c, end] = partial[c, end] + high[s, c, 0].astype(jnp.float32)
        second[0] = low[s, c, 1].astype(jnp.float32) + decode(kappa_low[s, c]) * weighted[c, 0]
        second[rows + 1] = high[s, c, 1].astype(jnp.float32) + decode(kappa_high[s, c]) * weighted[c, end]
        for r in range(rows):
            second[r + 1] = decode(kappa[s, c, r]) * partial[c, r]
        for r in range(rows):
            store(r, partial[c, r] + second[r] + second[r + 2] + along(second[r + 1]))

    def spot(q, c):
        return out_ref.at[:, pl.ds(pl.multiple_of(q * part + c * CHUNK, CHUNK), CHUNK), :]

    def give(s, c):
        return remote(main.at[s, c], spot(section, c), out_send.at[s, c], out_recv.at[section, c], (s, band))

    def taken(q, c):
        return remote(main.at[q, c], spot(q, c), out_send.at[q, c], out_recv.at[q, c], (q, band))

    def finish(s, c, r, value):
        main[s, c, r] = value.astype(jnp.bfloat16)

    def deliver(s, c):
        @pl.when(s != section)
        def _():
            give(s, c).start()

        @pl.when(s == section)
        def _():
            spot(section, c)[...] = main[s, c]

    last_from = lax.rem(section + 1, sections)

    @pl.when(last_from != 0)
    def _():
        kappa_arrival(last_from).wait_recv()

    for c in range(chunks):
        end_load(c).wait()

    def open_last(c, carry):
        begin(last, c)
        return carry

    lax.fori_loop(0, chunks, open_last, 0)

    order = iota((tile_len, tile_len), 0)
    other = iota((tile_len, tile_len), 1)

    def by_part(a, b, size):
        level = a // TW
        place_of = (level // size) * (size * TW) + lax.rem(a, TW) * size + lax.rem(level, size)
        return ones_where(place_of == b).astype(jnp.bfloat16)

    to_parts, from_parts = by_part(order, other, part), by_part(other, order, levels)

    state_land()
    top, rest = split(state_in[...].reshape(total, tile_len))
    own = dot(place_t[...], jnp.concatenate([top, rest], axis=1)).astype(jnp.bfloat16)
    top, rest = dot(own[:, :tile_len], from_parts), dot(own[:, tile_len:], from_parts)
    groups = blocks // PAD
    for g in range(groups):
        span = slice(g * PAD, (g + 1) * PAD)
        state_rows[g] = jnp.concatenate([top[span], rest[span]], axis=0).astype(jnp.bfloat16)
    among = lax.rem(iota((2 * PAD, tile_len), 0), PAD)

    def product(both, mats, g):
        picked = jnp.zeros((2 * PAD, tile_len), jnp.float32)
        for i in range(PAD):
            picked = jnp.where(among == i, dot(both, mats[g * PAD + i]), picked)
        return picked[:PAD] + picked[PAD:]

    for g in range(groups):
        here = slice(g * PAD, (g + 1) * PAD)
        pred = product(state_rows[g], jac_t, g)
        weight = weight_ref[here, :] * valid_ref[here, :].astype(jnp.float32)
        resid = weight * (value_ref[here, :] - pred)
        top = resid.astype(jnp.bfloat16).astype(jnp.float32)
        resid_rows[g] = jnp.concatenate([top, resid - top], axis=0).astype(jnp.bfloat16)
    for g in range(groups):
        terms[g * PAD : (g + 1) * PAD, :] = product(resid_rows[g], jac, g)
    top, rest = split(terms[...])
    top, rest = dot(top, to_parts).astype(jnp.bfloat16), dot(rest, to_parts).astype(jnp.bfloat16)
    sent = dot(place[...], top) + dot(place[...], rest)
    group = lats * PAD
    strip = iota((group, tile_len), 1) // width
    for q in range(sections):
        parcel = jnp.zeros((group, tile_len), jnp.float32)
        for s in range(sections):
            moved = sent[s * group : (s + 1) * group]
            if s != q:
                moved = pltpu.roll(moved, ((s - q) % sections) * width, 1)
            parcel = jnp.where(strip == s, moved, parcel)
        term_out[q * lats : (q + 1) * lats] = parcel.reshape(lats, PAD, tile_len)
    term_begin()
    ids_drain()
    state_drain()

    for j in range(sections):
        @pl.when(has_high)
        def _(j=j):
            from_high(j).wait_recv()

        @pl.when(has_low)
        def _(j=j):
            from_low(j).wait_recv()

    def kappa_land(j, carry):
        @pl.when(j != last_from)
        def _():
            kappa_arrival(j).wait_recv()

        return carry

    lax.fori_loop(1, sections, kappa_land, 0)

    def close_last(c, carry):
        def keep(r, value):
            early[c, r] = value

        complete(last, c, keep)
        return carry

    lax.fori_loop(0, chunks, close_last, 0)

    term_land()
    got = term_in[...].reshape(total, tile_len).T
    top = got.astype(jnp.bfloat16).astype(jnp.float32)
    rest = got - top
    for s in range(sections):
        span = slice(s * width, (s + 1) * width)
        stack = jnp.concatenate([top[span], rest[span]], axis=0).astype(jnp.bfloat16)
        terms_t[s] = stack
    wide = 2 * LANES
    parity = lax.rem(iota((part, wide), 1), TW)

    def scatter(s):
        left = terms_t[s]
        for r in range(rows):
            for c in range(nlon // wide):
                right = jnp.concatenate([tiles(s, r, 2 * c), tiles(s, r, 2 * c + 1)], axis=1)
                both = dot(left, right)
                both = both[:width] + both[width:]
                value = jnp.where(parity == 0, both[:part], both[part:])
                for k in range(chunks):
                    forcing[s, k, r, :, c * wide : (c + 1) * wide] = value[k * CHUNK : (k + 1) * CHUNK]

    scatter(last)

    def start_last(c, carry):
        for r in range(rows):
            finish(last, c, r, early[c, r] + forcing[last, c, r])
        if last > 0:
            begin(last - 1, c)
        deliver(last, c)
        return carry

    lax.fori_loop(0, chunks, start_last, 0)

    def scatter_other(j, carry):
        scatter(last - j)
        return carry

    lax.fori_loop(1, sections, scatter_other, 0)

    def go(i, carry):
        s = last - 1 - i // chunks
        c = lax.rem(i, chunks)
        complete(s, c, lambda r, value: finish(s, c, r, value + forcing[s, c, r]))

        @pl.when(s > 0)
        def _():
            begin(s - 1, c)

        deliver(s, c)
        return carry

    lax.fori_loop(0, last * chunks, go, 0)

    term_drain()
    for j in range(1, sections):
        kappa_copy(j).wait_send()
    for cond, copy in ((has_low, row_down), (has_high, row_up)):
        @pl.when(cond)
        def _(copy=copy):
            for j in range(sections):
                copy(j).wait_send()

    def settle(i, carry):
        s, c = i // chunks, lax.rem(i, chunks)

        @pl.when(has_low)
        def _():
            downward(s, c).wait_send()

        @pl.when(has_high)
        def _():
            upward(s, c).wait_send()

        @pl.when(s != section)
        def _():
            give(s, c).wait_send()

        return carry

    lax.fori_loop(0, sections * chunks, settle, 0)

    def gain(i, carry):
        q, c = lax.rem(section + 1 + i // chunks, sections), lax.rem(i, chunks)
        taken(q, c).wait_recv()
        return carry

    lax.fori_loop(0, last * chunks, gain, 0)


def sweep(owner, tile, value, weight, valid, traj, coeff, end, jac, slots):
    lats, sections = lax.axis_size("lat"), lax.axis_size("tm")
    count = sections * lats
    _, rows, levels, nlon = traj.shape
    blocks = owner.shape[1]
    tile_len = levels * TW
    total = count * PAD
    chunks = levels // sections // CHUNK
    bf16, f32 = jnp.bfloat16, jnp.float32
    parcels = pltpu.VMEM((count, PAD, tile_len), f32)
    stacked = pltpu.VMEM((blocks // PAD, 2 * PAD, tile_len), bf16)
    work = pltpu.VMEM((chunks, rows, CHUNK, nlon), f32)
    edges = pltpu.VMEM((sections, chunks, SUB, CHUNK, nlon), bf16)
    codes = lambda *lead: pltpu.VMEM(lead + (CHUNK, nlon), jnp.int16)
    hbm = pl.BlockSpec(memory_space=pltpu.HBM)
    dma = pltpu.SemaphoreType.DMA
    return pl.pallas_call(
        functools.partial(sweep_kernel, lats, sections, slots),
        out_shape=jax.ShapeDtypeStruct((rows, levels, nlon), bf16),
        in_specs=[hbm] * 9,
        out_specs=VMEM,
        scratch_shapes=[
            pltpu.VMEM(owner.shape, owner.dtype),
            pltpu.VMEM(tile.shape, tile.dtype),
            pltpu.VMEM(value.shape, value.dtype),
            pltpu.VMEM(weight.shape, weight.dtype),
            pltpu.VMEM(valid.shape, valid.dtype),
            pltpu.VMEM((rows, levels, nlon), f32),
            pltpu.VMEM((rows, levels, nlon), f32),
            pltpu.VMEM(jac.shape, bf16),
            pltpu.VMEM(jac.shape, bf16),
            pltpu.VMEM((rows, nlon, 2 * tile_len), bf16),
            pltpu.VMEM((rows, total, nlon), bf16),
            pltpu.VMEM((total, blocks), bf16),
            pltpu.VMEM((blocks, total), bf16),
            pltpu.VMEM((sections, total, LANES), bf16),
            pltpu.VMEM((sections, total, LANES), bf16),
            pltpu.VMEM((lats, 1, LANES), f32),
            pltpu.VMEM((count, 1, LANES), f32),
            parcels, parcels, parcels, parcels, stacked, stacked,
            pltpu.VMEM((blocks, tile_len), f32),
            pltpu.VMEM((sections, 2 * tile_len // sections, total), bf16),
            codes(sections, chunks, rows),
            codes(sections, chunks, rows),
            codes(sections, chunks),
            codes(sections, chunks),
            pltpu.VMEM((sections + 1, chunks, rows, CHUNK, nlon), bf16),
            pltpu.VMEM((sections, chunks, rows, CHUNK, nlon), f32),
            work, work,
            pltpu.VMEM((rows + 2, CHUNK, nlon), f32),
            work,
            edges, edges, edges, edges,
            dma((8,)),
            dma((chunks,)),
        ]
        + [dma((count,))] * 6
        + [dma((sections,))] * 6
        + [dma((sections, chunks))] * 6,
        compiler_params=pltpu.CompilerParams(
            collective_id=1, has_side_effects=True, vmem_limit_bytes=63 * 1024 * 1024
        ),
        name="sweep",
    )(owner, tile, value, weight, valid, traj, coeff, end, jac)


def per_device(
    trajectory,
    diffusivity,
    adjoint_end,
    obs_jac,
    obs_value,
    obs_weight,
    obs_valid,
    obs_owner,
    obs_tile,
):
    devices = lax.axis_size("tm") * lax.axis_size("lat")
    blocks = obs_owner.shape[0]
    slots = max(2, 2 * blocks // devices)
    rounded = sweep(
        obs_owner[:, 0][None, :], obs_tile[None, :], obs_value, obs_weight, obs_valid,
        trajectory, diffusivity, adjoint_end, obs_jac, slots,
    )
    return rounded.astype(jnp.float32)[None]


def solution(mesh):
    in_specs = (
        P("tm", "lat", None, None),
        P("tm", "lat", None, None),
        P("lat", None, None),
        P(("tm", "lat"), None, None),
        P(("tm", "lat"), None),
        P(("tm", "lat"), None),
        P(("tm", "lat"), None),
        P(("tm", "lat"), None),
        P(("tm", "lat")),
    )
    out_specs = P("tm", "lat", None, None)
    return jax.shard_map(
        per_device, mesh=mesh, in_specs=in_specs, out_specs=out_specs, check_vma=False
    )
```

time: 88.8 us -> 63.7 us (0.72)
  Pallas kernels: 83.2 us -> 60.8 us
  local copies, waits for them, and re-layouts: 5.3 us -> 0 us
  other arithmetic: 0 us -> 2.79 us
    pallas_call x2 -> x1, Pallas kernels: 83.2 us -> 60.8 us  [sweep(): pl.pallas_call(functools.partial(sweep_kernel, lats, sections, slots), ou...]
    unnamed x11 -> x0, local copies, waits for them, and re-layouts: 5.3 us -> none
    broadcast_in_dim x0 -> x1, other arithmetic: none -> 2.79 us  [per_device(): return rounded.astype(jnp.float32)[None]]
where the time goes in v2:
time: 63.7 us; the launch traced here: 63.6 us
  Pallas kernels  60.8 us (95%)
  other arithmetic  2.79 us (4%)
    pallas_call x1, Pallas kernels, sweep(): pl.pallas_call(functools.partial(sweep_kernel, lats, sections, slots), ou...  60.8 us
    broadcast_in_dim x1, other arithmetic, per_device(): return rounded.astype(jnp.float32)[None]  2.79 us

profile of v2, /device:TPU:8, one launch (start us, length us, event | category | flops | bytes accessed | tf_op | source)
XLA Modules:
  0.0 63.6 jit_solution(6992574267293800795)
XLA Ops:
  0.0 60.8 %sweep.1 = bf16[4,64,2048]{2,1,0:T(8,128)(2,1)} custom-call(s32[1,96]{1,0:T(1,128)} %bitcast.5, s32[1,96]{1,0:T(1,128)} %bitcast.6, f32[96,128]{1,0:T(8,128)} %value_hbm.1, f32[96,128]{1,0:T(8,128)} %weight_hbm.1, s32[96,128]{1,0:T(8,128)} %valid_hbm.1, f32[1,4,64,2048]{3,2,1,0:T(8,128)} %traj_hbm.1, f32[1,4,64,2048]{3,2,1,0:T(8,128)} %coeff_hbm.1, ...), custom_call_target="tpu_custom_call" | custom-call | tf_op jit(solution)/shard_map/sweep/pallas_call | solution.py:564
  60.8 2.8 %bitcast_convert_fusion = f32[1,4,64,2048]{3,2,1,0:T(8,128)} fusion(bf16[4,64,2048]{2,1,0:T(8,128)(2,1)} %sweep.1), kind=kLoop, calls=%fused_computation | loop fusion | flops 524288 | bytes 3145728 | tf_op jit(solution)/shard_map/broadcast_in_dim | solution.py:631

commit v3 on v2

--- a/solution.py
+++ b/solution.py
@@ -44,7 +44,7 @@
     edge_low, edge_high, low, high,
     load_sem, end_sem, ids_send, ids_recv, state_send, state_recv, term_send, term_recv,
     kappa_send, kappa_recv, down_send, down_recv, up_send, up_recv,
-    low_send, low_recv, high_send, high_recv, out_send, out_recv,
+    low_send, low_recv, high_send, high_recv, out_send, out_recv, own_sem,
 ):
     section, band = lax.axis_index("tm"), lax.axis_index("lat")
     count = sections * lats
@@ -97,14 +97,14 @@
             src_ref=src, dst_ref=dst, send_sem=send, recv_sem=recv, device_id=where, device_id_type=MESH
         )
 
-    def swap(pick, into, send, recv):
+    def swap(pick, into, send, recv, used):
         def outgoing(j):
             to, where = peer(j)
-            return remote(pick(to), into.at[me], send.at[j], recv.at[j], where)
+            return remote(pick(to).at[:used], into.at[me, :used], send.at[j], recv.at[j], where)
 
         def incoming(j):
             source, where = peer(count - j)
-            return remote(pick(source), into.at[source], send.at[j], recv.at[j], where)
+            return remote(pick(source).at[:used], into.at[source, :used], send.at[j], recv.at[j], where)
 
         def launch(j, carry):
             outgoing(j).start()
@@ -124,9 +124,9 @@
 
         return begin, lambda: lax.fori_loop(1, count, land, 0), lambda: lax.fori_loop(1, count, drain, 0)
 
-    ids_begin, ids_land, ids_drain = swap(lambda d: ids_out.at[lax.rem(d, lats)], ids_in, ids_send, ids_recv)
-    state_begin, state_land, state_drain = swap(lambda d: state_out.at[d], state_in, state_send, state_recv)
-    term_begin, term_land, term_drain = swap(lambda d: term_out.at[d], term_in, term_send, term_recv)
+    ids_begin, ids_land, ids_drain = swap(lambda d: ids_out.at[lax.rem(d, lats)], ids_in, ids_send, ids_recv, 1)
+    state_begin, state_land, state_drain = swap(lambda d: state_out.at[d], state_in, state_send, state_recv, slots)
+    term_begin, term_land, term_drain = swap(lambda d: term_out.at[d], term_in, term_send, term_recv, slots)
 
     for load in loads[:2]:
         load.wait()
@@ -151,6 +151,8 @@
         lists = lists + pltpu.roll(packed[s * lats : (s + 1) * lats], s * 2 * PAD, 1)
     for b in range(lats):
         ids_out[b] = lists[b : b + 1]
+    state_in[...] = jnp.zeros_like(state_in)
+    term_in[...] = jnp.zeros_like(term_in)
     pl.semaphore_wait(barrier, count - 1)
     ids_begin()
 
@@ -178,18 +180,19 @@
         source = lax.rem(section + sections - j, sections)
         return remote(coded.at[source, :, 0], kappa_low.at[source], up_send.at[j], up_recv.at[j], (source, band))
 
-    def share():
+    def share_kappa():
         for j in range(1, sections):
             kappa_copy(j).start()
 
+    def share_rows(first, stop):
         @pl.when(has_low)
         def _():
-            for j in range(sections):
+            for j in range(first, stop):
                 row_down(j).start()
 
         @pl.when(has_high)
         def _():
-            for j in range(sections):
+            for j in range(first, stop):
                 row_up(j).start()
 
     loads[2].wait()
@@ -207,7 +210,12 @@
 
     @pl.when(is_odd)
     def _():
-        share()
+        share_kappa()
+        share_rows(0, sections)
+
+    @pl.when(jnp.logical_not(is_odd))
+    def _():
+        share_rows(0, 1)
 
     kappa[section] = coded[section]
 
@@ -225,6 +233,16 @@
         high[...] = jnp.zeros_like(high)
         kappa_high[...] = jnp.zeros_like(kappa_high)
 
+    order = iota((tile_len, tile_len), 0)
+    other = iota((tile_len, tile_len), 1)
+
+    def by_part(a, b, size):
+        level = a // TW
+        place_of = (level // size) * (size * TW) + lax.rem(a, TW) * size + lax.rem(level, size)
+        return ones_where(place_of == b).astype(jnp.bfloat16)
+
+    to_parts, from_parts = by_part(order, other, part), by_part(other, order, levels)
+
     loads[3].wait()
     even = lax.rem(iota((levels, nlon), 1), TW)
 
@@ -232,7 +250,10 @@
         values = traj[r]
         top = values.astype(jnp.bfloat16).astype(jnp.float32)
         parts = [jnp.where(even == p, x, 0.0) for x in (top, values - top) for p in range(TW)]
-        fields[r] = jnp.concatenate(parts, axis=0).T.astype(jnp.bfloat16)
+        stack = jnp.concatenate(parts, axis=0).T.astype(jnp.bfloat16)
+        fields[r] = jnp.concatenate(
+            [dot(stack[:, :tile_len], from_parts), dot(stack[:, tile_len:], from_parts)], axis=1
+        ).astype(jnp.bfloat16)
         return carry
 
     lax.fori_loop(0, rows, field, 0)
@@ -268,7 +289,8 @@
 
     @pl.when(jnp.logical_not(is_odd))
     def _():
-        share()
+        share_kappa()
+        share_rows(1, sections)
 
     for load in loads[4:]:
         load.wait()
@@ -298,28 +320,36 @@
         return x.astype(jnp.int32).astype(jnp.float32) * (1.0 / SCALE)
 
     def begin(s, c):
-        for r in range(rows):
+        end = rows - 1
+
+        def weigh(r):
             weighted[c, r] = decode(kappa[s, c, r]) * main[s + 1, c, r].astype(jnp.float32)
-        for r in range(rows):
-            mid = weighted[c, r]
-            value = main[s + 1, c, r].astype(jnp.float32) + along(mid)
+
+        def inner(r):
+            value = main[s + 1, c, r].astype(jnp.float32) + along(weighted[c, r])
             if r > 0:
                 value = value + weighted[c, r - 1]
-            if r < rows - 1:
+            if r < end:
                 value = value + weighted[c, r + 1]
             partial[c, r] = value
-            for at, ref in ((0, edge_low), (rows - 1, edge_high)):
-                if r == at:
-                    ref[s, c, 0] = mid.astype(jnp.bfloat16)
-                    ref[s, c, 1] = (decode(kappa[s, c, r]) * value).astype(jnp.bfloat16)
-
-        @pl.when(has_low)
-        def _():
-            downward(s, c).start()
-
-        @pl.when(has_high)
-        def _():
-            upward(s, c).start()
+
+        for r, near, ref, there, copy in (
+            (0, 1, edge_low, has_low, downward), (end, end - 1, edge_high, has_high, upward)
+        ):
+            weigh(r)
+            weigh(near)
+            inner(r)
+            ref[s, c, 0] = weighted[c, r].astype(jnp.bfloat16)
+            ref[s, c, 1] = (decode(kappa[s, c, r]) * partial[c, r]).astype(jnp.bfloat16)
+
+            @pl.when(there)
+            def _(copy=copy):
+                copy(s, c).start()
+
+        for r in range(2, end - 1):
+            weigh(r)
+        for r in range(1, end):
+            inner(r)
 
     def complete(s, c, store):
         @pl.when(has_low)
@@ -340,14 +370,18 @@
         for r in range(rows):
             store(r, partial[c, r] + second[r] + second[r + 2] + along(second[r + 1]))
 
-    def spot(q, c):
-        return out_ref.at[:, pl.ds(pl.multiple_of(q * part + c * CHUNK, CHUNK), CHUNK), :]
-
-    def give(s, c):
-        return remote(main.at[s, c], spot(section, c), out_send.at[s, c], out_recv.at[section, c], (s, band))
-
-    def taken(q, c):
-        return remote(main.at[q, c], spot(q, c), out_send.at[q, c], out_recv.at[q, c], (q, band))
+    def spot(q, c, r):
+        return out_ref.at[r, pl.ds(pl.multiple_of(q * part + c * CHUNK, CHUNK), CHUNK), :]
+
+    def give(s, c, r):
+        where = (s, band)
+        return remote(main.at[s, c, r], spot(section, c, r), out_send.at[s, c, r], out_recv.at[section, c, r], where)
+
+    def taken(q, c, r):
+        return remote(main.at[q, c, r], spot(q, c, r), out_send.at[q, c, r], out_recv.at[q, c, r], (q, band))
+
+    def keep_own(c, r):
+        return pltpu.make_async_copy(main.at[section, c, r], spot(section, c, r), own_sem.at[c, r])
 
     def finish(s, c, r, value):
         main[s, c, r] = value.astype(jnp.bfloat16)
@@ -355,11 +389,13 @@
     def deliver(s, c):
         @pl.when(s != section)
         def _():
-            give(s, c).start()
+            for r in range(rows):
+                give(s, c, r).start()
 
         @pl.when(s == section)
         def _():
-            spot(section, c)[...] = main[s, c]
+            for r in range(rows):
+                keep_own(c, r).start()
 
     last_from = lax.rem(section + 1, sections)
 
@@ -376,20 +412,9 @@
 
     lax.fori_loop(0, chunks, open_last, 0)
 
-    order = iota((tile_len, tile_len), 0)
-    other = iota((tile_len, tile_len), 1)
-
-    def by_part(a, b, size):
-        level = a // TW
-        place_of = (level // size) * (size * TW) + lax.rem(a, TW) * size + lax.rem(level, size)
-        return ones_where(place_of == b).astype(jnp.bfloat16)
-
-    to_parts, from_parts = by_part(order, other, part), by_part(other, order, levels)
-
     state_land()
     top, rest = split(state_in[...].reshape(total, tile_len))
-    own = dot(place_t[...], jnp.concatenate([top, rest], axis=1)).astype(jnp.bfloat16)
-    top, rest = dot(own[:, :tile_len], from_parts), dot(own[:, tile_len:], from_parts)
+    top, rest = dot(place_t[...], top), dot(place_t[...], rest)
     groups = blocks // PAD
     for g in range(groups):
         span = slice(g * PAD, (g + 1) * PAD)
@@ -531,7 +556,13 @@
 
         @pl.when(s != section)
         def _():
-            give(s, c).wait_send()
+            for r in range(rows):
+                give(s, c, r).wait_send()
+
+        @pl.when(s == section)
+        def _():
+            for r in range(rows):
+                keep_own(c, r).wait()
 
         return carry
 
@@ -539,7 +570,8 @@
 
     def gain(i, carry):
         q, c = lax.rem(section + 1 + i // chunks, sections), lax.rem(i, chunks)
-        taken(q, c).wait_recv()
+        for r in range(rows):
+            taken(q, c, r).wait_recv()
         return carry
 
     lax.fori_loop(0, last * chunks, gain, 0)
@@ -565,7 +597,7 @@
         functools.partial(sweep_kernel, lats, sections, slots),
         out_shape=jax.ShapeDtypeStruct((rows, levels, nlon), bf16),
         in_specs=[hbm] * 9,
-        out_specs=VMEM,
+        out_specs=hbm,
         scratch_shapes=[
             pltpu.VMEM(owner.shape, owner.dtype),
             pltpu.VMEM(tile.shape, tile.dtype),
@@ -602,12 +634,47 @@
         ]
         + [dma((count,))] * 6
         + [dma((sections,))] * 6
-        + [dma((sections, chunks))] * 6,
+        + [dma((sections, chunks))] * 4
+        + [dma((sections, chunks, rows))] * 2
+        + [dma((chunks, rows))],
         compiler_params=pltpu.CompilerParams(
             collective_id=1, has_side_effects=True, vmem_limit_bytes=63 * 1024 * 1024
         ),
         name="sweep",
     )(owner, tile, value, weight, valid, traj, coeff, end, jac)
+
+
+def widen_kernel(x_hbm, out_hbm, x, wide, in_sem, out_sem):
+    rows = x.shape[0]
+
+    def load(r):
+        return pltpu.make_async_copy(x_hbm.at[r], x.at[r], in_sem.at[r])
+
+    def save(r):
+        return pltpu.make_async_copy(wide.at[r], out_hbm.at[0, r], out_sem.at[r])
+
+    for r in range(rows):
+        load(r).start()
+    for r in range(rows):
+        load(r).wait()
+        wide[r] = x[r].astype(jnp.float32)
+        save(r).start()
+    for r in range(rows):
+        save(r).wait()
+
+
+def widen(x):
+    hbm = pl.BlockSpec(memory_space=pltpu.HBM)
+    dma = pltpu.SemaphoreType.DMA((x.shape[0],))
+    return pl.pallas_call(
+        widen_kernel,
+        out_shape=jax.ShapeDtypeStruct((1,) + x.shape, jnp.float32),
+        in_specs=[hbm],
+        out_specs=hbm,
+        scratch_shapes=[pltpu.VMEM(x.shape, x.dtype), pltpu.VMEM(x.shape, jnp.float32), dma, dma],
+        compiler_params=pltpu.CompilerParams(vmem_limit_bytes=63 * 1024 * 1024),
+        name="widen",
+    )(x)
 
 
 def per_device(
@@ -628,7 +695,7 @@
         obs_owner[:, 0][None, :], obs_tile[None, :], obs_value, obs_weight, obs_valid,
         trajectory, diffusivity, adjoint_end, obs_jac, slots,
     )
-    return rounded.astype(jnp.float32)[None]
+    return widen(rounded)
 
 
 def solution(mesh):

time: 63.7 us -> 62 us (0.973)
  other arithmetic: 2.79 us -> 0 us
  Pallas kernels: 60.8 us -> 61.8 us
    broadcast_in_dim x1 -> x0, other arithmetic: 2.79 us -> none  [per_device(): return rounded.astype(jnp.float32)[None]]
    pallas_call x0 -> x1, Pallas kernels: none -> 2.36 us  [widen(): pl.pallas_call(widen_kernel, out_shape=jax.ShapeDtypeStruct((1,) + x.shap...]
    pallas_call x1, Pallas kernels: 60.8 us -> 59.5 us  [sweep(): pl.pallas_call(functools.partial(sweep_kernel, lats, sections, slots), ou...]
where the time goes in v3:
time: 62 us; the launch traced here: 61.8 us
  Pallas kernels  61.8 us (100%)
    pallas_call x1, Pallas kernels, sweep(): pl.pallas_call(functools.partial(sweep_kernel, lats, sections, slots), ou...  59.5 us
    pallas_call x1, Pallas kernels, widen(): pl.pallas_call(widen_kernel, out_shape=jax.ShapeDtypeStruct((1,) + x.shap...  2.36 us

profile of v3, /device:TPU:8, one launch (start us, length us, event | category | flops | bytes accessed | tf_op | source)
XLA Modules:
  0.0 61.8 jit_solution(16425872858472126079)
XLA Ops:
  0.0 59.5 %sweep.1.x_hbm = bf16[4,64,2048]{2,1,0:T(8,128)(2,1)} custom-call(s32[1,96]{1,0:T(1,128)} %bitcast.2, s32[1,96]{1,0:T(1,128)} %bitcast.3, f32[96,128]{1,0:T(8,128)} %value_hbm.1, f32[96,128]{1,0:T(8,128)} %weight_hbm.1, s32[96,128]{1,0:T(8,128)} %valid_hbm.1, f32[1,4,64,2048]{3,2,1,0:T(8,128)} %traj_hbm.1, f32[1,4,64,2048]{3,2,1,0:T(8,128)} %coeff_hbm.1, ...), custom_call_target="tpu_custom_call" | custom-call | tf_op jit(solution)/shard_map/sweep/pallas_call | solution.py:596
  59.5 2.4 %widen.1 = f32[1,4,64,2048]{3,2,1,0:T(8,128)} custom-call(bf16[4,64,2048]{2,1,0:T(8,128)(2,1)} %sweep.1.x_hbm), custom_call_target="tpu_custom_call" | custom-call | tf_op jit(solution)/shard_map/widen/pallas_call | solution.py:669

commit v4 on v3

--- a/solution.py
+++ b/solution.py
@@ -86,11 +86,26 @@
         to = lax.rem(me + j, count)
         return to, (to // lats, lax.rem(to, lats))
 
-    def greet(j, carry):
-        pl.semaphore_signal(barrier, inc=1, device_id=peer(j)[1], device_id_type=MESH)
-        return carry
-
-    lax.fori_loop(1, count, greet, 0)
+    def nearer(i):
+        far = lats - 1 - i // 2
+        lat = jnp.where(lax.rem(i, 2) == 0, band + far, band - far)
+        return far, lat, (lat >= 0) & (lat < lats) & ((far > 0) | (lax.rem(i, 2) == 0))
+
+    def greet(i, carry):
+        far, lat, inside = nearer(i)
+
+        @pl.when(inside)
+        def _():
+            def one(j, carry):
+                where = (lax.rem(section + sections - j, sections), lat)
+                pl.semaphore_signal(barrier, inc=1, device_id=where, device_id_type=MESH)
+                return carry
+
+            lax.fori_loop(1, jnp.where(far > 0, sections + 1, sections), one, 0)
+
+        return carry
+
+    lax.fori_loop(0, 2 * lats, greet, 0)
 
     def remote(src, dst, send, recv, where):
         return pltpu.make_async_remote_copy(
@@ -98,28 +113,37 @@
         )
 
     def swap(pick, into, send, recv, used):
-        def outgoing(j):
-            to, where = peer(j)
-            return remote(pick(to).at[:used], into.at[me, :used], send.at[j], recv.at[j], where)
-
-        def incoming(j):
-            source, where = peer(count - j)
-            return remote(pick(source).at[:used], into.at[source, :used], send.at[j], recv.at[j], where)
-
-        def launch(j, carry):
-            outgoing(j).start()
+        def outgoing(to):
+            where = (to // lats, lax.rem(to, lats))
+            return remote(pick(to).at[:used], into.at[me, :used], send.at[to], recv.at[me], where)
+
+        def incoming(source):
+            where = (source // lats, lax.rem(source, lats))
+            return remote(pick(source).at[:used], into.at[source, :used], send.at[source], recv.at[source], where)
+
+        def launch(i, carry):
+            far, lat, inside = nearer(i)
+
+            @pl.when(inside)
+            def _():
+                def one(j, carry):
+                    outgoing(lax.rem(section + sections - j, sections) * lats + lat).start()
+                    return carry
+
+                lax.fori_loop(1, jnp.where(far > 0, sections + 1, sections), one, 0)
+
             return carry
 
         def land(j, carry):
-            incoming(j).wait_recv()
+            incoming(lax.rem(me + count - j, count)).wait_recv()
             return carry
 
         def drain(j, carry):
-            outgoing(j).wait_send()
+            outgoing(lax.rem(me + j, count)).wait_send()
             return carry
 
         def begin():
-            lax.fori_loop(1, count, launch, 0)
+            lax.fori_loop(0, 2 * lats, launch, 0)
             into[me] = pick(me)[...]
 
         return begin, lambda: lax.fori_loop(1, count, land, 0), lambda: lax.fori_loop(1, count, drain, 0)
@@ -301,12 +325,6 @@
 
     lax.fori_loop(0, blocks, turn, 0, unroll=4)
 
-    def list_other(j, carry):
-        listed(lax.rem(section + j, sections))
-        return carry
-
-    lax.fori_loop(1, sections, list_other, 0)
-
     def downward(s, c):
         return remote(edge_low.at[s, c], high.at[s, c], low_send.at[s, c], high_recv.at[s, c], (section, band - 1))
 
@@ -423,8 +441,11 @@
 
     def product(both, mats, g):
         picked = jnp.zeros((2 * PAD, tile_len), jnp.float32)
-        for i in range(PAD):
-            picked = jnp.where(among == i, dot(both, mats[g * PAD + i]), picked)
+        for i in range(0, PAD, 2):
+            k = g * PAD + i
+            full = dot(both, jnp.concatenate([mats[k], mats[k + 1]], axis=1))
+            picked = jnp.where(among == i, full[:, :tile_len], picked)
+            picked = jnp.where(among == i + 1, full[:, tile_len:], picked)
         return picked[:PAD] + picked[PAD:]
 
     for g in range(groups):
@@ -450,6 +471,12 @@
             parcel = jnp.where(strip == s, moved, parcel)
         term_out[q * lats : (q + 1) * lats] = parcel.reshape(lats, PAD, tile_len)
     term_begin()
+    def list_other(j, carry):
+        listed(lax.rem(section + j, sections))
+        return carry
+
+    lax.fori_loop(1, sections, list_other, 0)
+
     ids_drain()
     state_drain()
 

time: 62 us -> 59.7 us (0.963)
  Pallas kernels: 61.8 us -> 59.5 us
    pallas_call x1, Pallas kernels: 59.5 us -> 57.2 us  [sweep(): pl.pallas_call(functools.partial(sweep_kernel, lats, sections, slots), ou...]
where the time goes in v4:
time: 59.7 us; the launch traced here: 59.6 us
  Pallas kernels  59.5 us (100%)
    pallas_call x1, Pallas kernels, sweep(): pl.pallas_call(functools.partial(sweep_kernel, lats, sections, slots), ou...  57.2 us
    pallas_call x1, Pallas kernels, widen(): pl.pallas_call(widen_kernel, out_shape=jax.ShapeDtypeStruct((1,) + x.shap...  2.36 us

profile of v4, /device:TPU:8, one launch (start us, length us, event | category | flops | bytes accessed | tf_op | source)
XLA Modules:
  0.0 59.6 jit_solution(7349311856444627702)
XLA Ops:
  0.0 57.2 %sweep.1.x_hbm = bf16[4,64,2048]{2,1,0:T(8,128)(2,1)} custom-call(s32[1,96]{1,0:T(1,128)} %bitcast.2, s32[1,96]{1,0:T(1,128)} %bitcast.3, f32[96,128]{1,0:T(8,128)} %value_hbm.1, f32[96,128]{1,0:T(8,128)} %weight_hbm.1, s32[96,128]{1,0:T(8,128)} %valid_hbm.1, f32[1,4,64,2048]{3,2,1,0:T(8,128)} %traj_hbm.1, f32[1,4,64,2048]{3,2,1,0:T(8,128)} %coeff_hbm.1, ...), custom_call_target="tpu_custom_call" | custom-call | tf_op jit(solution)/shard_map/sweep/pallas_call | solution.py:623
  57.2 2.4 %widen.1 = f32[1,4,64,2048]{3,2,1,0:T(8,128)} custom-call(bf16[4,64,2048]{2,1,0:T(8,128)(2,1)} %sweep.1.x_hbm), custom_call_target="tpu_custom_call" | custom-call | tf_op jit(solution)/shard_map/widen/pallas_call | solution.py:696

commit v5 on v4

--- a/solution.py
+++ b/solution.py
@@ -205,7 +205,7 @@
         return remote(coded.at[source, :, 0], kappa_low.at[source], up_send.at[j], up_recv.at[j], (source, band))
 
     def share_kappa():
-        for j in range(1, sections):
+        for j in range(sections - 1, 0, -1):
             kappa_copy(j).start()
 
     def share_rows(first, stop):
@@ -337,7 +337,7 @@
     def decode(x):
         return x.astype(jnp.int32).astype(jnp.float32) * (1.0 / SCALE)
 
-    def begin(s, c):
+    def begin(s, c, steps=(0, 1, 2)):
         end = rows - 1
 
         def weigh(r):
@@ -351,9 +351,11 @@
                 value = value + weighted[c, r + 1]
             partial[c, r] = value
 
-        for r, near, ref, there, copy in (
-            (0, 1, edge_low, has_low, downward), (end, end - 1, edge_high, has_high, upward)
+        for step, r, near, ref, there, copy in (
+            (0, 0, 1, edge_low, has_low, downward), (1, end, end - 1, edge_high, has_high, upward)
         ):
+            if step not in steps:
+                continue
             weigh(r)
             weigh(near)
             inner(r)
@@ -364,6 +366,8 @@
             def _(copy=copy):
                 copy(s, c).start()
 
+        if 2 not in steps:
+            return
         for r in range(2, end - 1):
             weigh(r)
         for r in range(1, end):
@@ -518,9 +522,9 @@
     wide = 2 * LANES
     parity = lax.rem(iota((part, wide), 1), TW)
 
-    def scatter(s):
+    def scatter(s, some):
         left = terms_t[s]
-        for r in range(rows):
+        for r in some:
             for c in range(nlon // wide):
                 right = jnp.concatenate([tiles(s, r, 2 * c), tiles(s, r, 2 * c + 1)], axis=1)
                 both = dot(left, right)
@@ -529,20 +533,27 @@
                 for k in range(chunks):
                     forcing[s, k, r, :, c * wide : (c + 1) * wide] = value[k * CHUNK : (k + 1) * CHUNK]
 
-    scatter(last)
-
-    def start_last(c, carry):
-        for r in range(rows):
-            finish(last, c, r, early[c, r] + forcing[last, c, r])
-        if last > 0:
-            begin(last - 1, c)
+    half = rows // 2
+    for some, steps in ((range(half), (0,)), (range(half, rows), (1, 2))):
+        scatter(last, some)
+
+        def start_last(c, carry, some=some, steps=steps):
+            for r in some:
+                finish(last, c, r, early[c, r] + forcing[last, c, r])
+            if last > 0:
+                begin(last - 1, c, steps)
+            return carry
+
+        lax.fori_loop(0, chunks, start_last, 0)
+
+    def give_last(c, carry):
         deliver(last, c)
         return carry
 
-    lax.fori_loop(0, chunks, start_last, 0)
+    lax.fori_loop(0, chunks, give_last, 0)
 
     def scatter_other(j, carry):
-        scatter(last - j)
+        scatter(last - j, range(rows))
         return carry
 
     lax.fori_loop(1, sections, scatter_other, 0)

time: 59.7 us -> 59.6 us (level)
  no operation moved by 1% of the time
where the time goes in v5:
time: 59.6 us; the launch traced here: 59.4 us
  Pallas kernels  59.4 us (100%)
    pallas_call x1, Pallas kernels, sweep(): pl.pallas_call(functools.partial(sweep_kernel, lats, sections, slots), ou...  57.1 us
    pallas_call x1, Pallas kernels, widen(): pl.pallas_call(widen_kernel, out_shape=jax.ShapeDtypeStruct((1,) + x.shap...  2.36 us

profile of v5, /device:TPU:8, one launch (start us, length us, event | category | flops | bytes accessed | tf_op | source)
XLA Modules:
  0.0 59.4 jit_solution(8442012636038074881)
XLA Ops:
  0.0 57.1 %sweep.1.x_hbm = bf16[4,64,2048]{2,1,0:T(8,128)(2,1)} custom-call(s32[1,96]{1,0:T(1,128)} %bitcast.2, s32[1,96]{1,0:T(1,128)} %bitcast.3, f32[96,128]{1,0:T(8,128)} %value_hbm.1, f32[96,128]{1,0:T(8,128)} %weight_hbm.1, s32[96,128]{1,0:T(8,128)} %valid_hbm.1, f32[1,4,64,2048]{3,2,1,0:T(8,128)} %traj_hbm.1, f32[1,4,64,2048]{3,2,1,0:T(8,128)} %coeff_hbm.1, ...), custom_call_target="tpu_custom_call" | custom-call | tf_op jit(solution)/shard_map/sweep/pallas_call | solution.py:634
  57.1 2.4 %widen.1 = f32[1,4,64,2048]{3,2,1,0:T(8,128)} custom-call(bf16[4,64,2048]{2,1,0:T(8,128)(2,1)} %sweep.1.x_hbm), custom_call_target="tpu_custom_call" | custom-call | tf_op jit(solution)/shard_map/widen/pallas_call | solution.py:707
